TPU v7x, 32 devices: a whole 2x2x4 slice. The times are simulated.
32 devices in a mesh: section: 2 (over core), seq: 16 (over z, y, x).
Axes of the slice: x: 2, y: 2, z: 4, core: 2. Of those that a mesh axis runs over, the one named last changes fastest.
Arguments:
- acts: bfloat16 [2, 4096, 2048], P('section', 'seq'), may hold values from -6 to 6
- in_proj: bfloat16 [2, 2048, 4640], P('section', 'seq'), may hold values from -0.125 to 0.125
- out_proj: bfloat16 [2, 2048, 2048], P('section'), may hold values from -0.125 to 0.125
- conv_weight: float32 [2, 4, 2304], P('section'), may hold values from -3 to 3
- conv_bias: float32 [2, 2304], P('section'), may hold values from -3 to 3
- dt_bias: float32 [2, 32], P('section'), may hold values from -4 to -1
- decay_rate: float32 [2, 32], P('section'), may hold values from 0.0001 to 0.5
- skip_gain: float32 [2, 32], P('section'), may hold values from -4 to 4
- level_bias: float32 [2, 256], P('section'), may hold values from -4 to 4
- norm_gain: float32 [2, 2048], P('section'), may hold values from 0.5 to 1.5
- gate_gain: float32 [2, 2048], P('section'), may hold values from 0.5 to 1.5
Outputs:
- handoff: bfloat16 [2, 4096, 2048], P('section', 'seq')
All inputs are finite; a program needn't handle non-finite values.
Results may differ from a plain program's by a relative error of at most 0.006.
Values may be sent and summed in bfloat16 or wider, within the bound.
A program may use at most 128 MiB of HBM per device.

v0:
```python
import jax
import jax.numpy as jnp
from jax import lax
from jax.sharding import PartitionSpec as P

EPS = 1e-05
best_precision = lax.Precision.HIGHEST


def swapped(block, axis, apart):
    count = lax.axis_size(axis)
    route = []
    for low in range(count):
        high = low | 1 << apart
        if high != low and high < count:
            route += [(low, high), (high, low)]
    return lax.ppermute(block, axis, route)


def from_behind(block, axis, distance):
    devices = range(lax.axis_size(axis))
    route = [(i - distance, i) for i in devices if i - distance in devices]
    return lax.ppermute(block, axis, route)


def passed_along(value, axis, steps):
    count = lax.axis_size(axis)
    pairs = [(source, (source + steps) % count) for source in range(count)]
    return lax.ppermute(value, axis, pairs)


def block_core(c_block, b_block, x_block, cum_block, dt_block, lam_block):
    length = c_block.shape[0]
    scores = jnp.dot(
        c_block, b_block.T, precision=best_precision, preferred_element_type=jnp.float32
    )
    row_ids = lax.broadcasted_iota(jnp.int32, (length, length), 0)
    col_ids = lax.broadcasted_iota(jnp.int32, (length, length), 1)
    causal = (col_ids <= row_ids)[:, :, None]
    differ = cum_block[:, None, :] - cum_block[None, :, :]
    decays = jnp.where(causal, jnp.exp(jnp.where(causal, differ, 0.0)), 0.0)
    weights = decays * scores[:, :, None] * dt_block[None, :, :] * lam_block[:, None, :]
    return jnp.einsum("tsh,shp->thp", weights, x_block, precision=best_precision)


def level_states(b_mat, values, cum, steps):
    tail = jnp.exp(cum[-1][None, :] - cum) * steps
    local_state = jnp.einsum(
        "sn,shp->hnp", b_mat, values * tail[:, :, None], precision=best_precision
    )
    position = lax.axis_index("seq")
    levels_used = lax.axis_size("seq").bit_length() - 1
    block_log = cum[-1]
    block_state = local_state
    before_log = jnp.zeros_like(block_log)
    buckets = []
    for level_bit in range(levels_used):
        other_log, other_state = swapped((block_log, block_state), "seq", level_bit)
        upper = position >> level_bit & 1 == 1
        buckets.append(jnp.where(upper, jnp.exp(before_log)[:, None, None] * other_state, 0.0))
        merged_upper = jnp.exp(block_log)[:, None, None] * other_state + block_state
        merged_lower = jnp.exp(other_log)[:, None, None] * block_state + other_state
        block_state = jnp.where(upper, merged_upper, merged_lower)
        before_log = jnp.where(upper, before_log + other_log, before_log)
        block_log = block_log + other_log
    return (jnp.stack(buckets, axis=0), levels_used)


def cross_terms(c_mat, stacked, levels_used, cum, lam):
    reads = jnp.einsum("tn,lhnp->tlhp", c_mat, stacked, precision=best_precision)
    scale = lam[:, :, 1 : levels_used + 1] * jnp.exp(cum)[:, :, None]
    return jnp.einsum("thl,tlhp->thp", scale, reads, precision=best_precision)


def per_device(
    acts,
    in_proj,
    out_proj,
    conv_weight,
    conv_bias,
    dt_bias,
    decay_rate,
    skip_gain,
    level_bias,
    norm_gain,
    gate_gain,
):
    hidden = acts[0].astype(jnp.float32)
    length = hidden.shape[0]
    inner = gate_gain.shape[1]
    heads = dt_bias.shape[1]
    head_size = inner // heads
    chans = conv_weight.shape[2]
    state_size = (chans - inner) // 2
    kernel_len = conv_weight.shape[1]
    margin = kernel_len - 1
    levels_all = level_bias.shape[1] // heads
    normed_in = (
        hidden * lax.rsqrt(jnp.mean(hidden * hidden, axis=1, keepdims=True) + EPS) * norm_gain[0]
    ).astype(jnp.bfloat16)
    projected = jnp.dot(
        normed_in,
        lax.all_gather(in_proj[0], "seq", axis=0, tiled=True),
        preferred_element_type=jnp.float32,
    )
    projected = projected.astype(jnp.bfloat16)
    own_rows = projected[:, :chans]
    earlier_rows = from_behind(own_rows[length - margin :], "seq", 1)
    conv_in = jnp.concatenate([earlier_rows, own_rows], axis=0).astype(jnp.float32)
    mixed = conv_bias[0] + jnp.zeros((length, chans), jnp.float32)
    for offset in range(kernel_len):
        mixed = mixed + conv_weight[0, offset] * conv_in[offset : offset + length]
    mixed = jax.nn.silu(mixed)
    values = mixed[:, :inner].reshape(length, heads, head_size)
    b_mat = mixed[:, inner : inner + state_size]
    c_mat = mixed[:, inner + state_size :]
    z_gate = projected[:, chans : chans + inner].astype(jnp.float32)
    steps = jax.nn.softplus(
        projected[:, chans + inner : chans + inner + heads].astype(jnp.float32) + dt_bias[0]
    )
    lam = jax.nn.softplus(
        projected[:, chans + inner + heads :].astype(jnp.float32) + level_bias[0]
    ).reshape(length, heads, levels_all)
    cum = jnp.cumsum(-steps * decay_rate[0], axis=0)
    inside = block_core(c_mat, b_mat, values, cum, steps, lam[:, :, 0])
    stacked, levels_used = level_states(b_mat, values, cum, steps)
    outside = cross_terms(c_mat, stacked, levels_used, cum, lam)
    y_heads = inside + outside + skip_gain[0][None, :, None] * values
    y_flat = y_heads.reshape(length, inner)
    gated = y_flat * jax.nn.silu(z_gate)
    normed = (
        gated * lax.rsqrt(jnp.mean(gated * gated, axis=1, keepdims=True) + EPS) * gate_gain[0]
    ).astype(jnp.bfloat16)
    result = (hidden + jnp.dot(normed, out_proj[0], preferred_element_type=jnp.float32)).astype(
        jnp.bfloat16
    )
    moved = passed_along(result, "section", 1)
    return moved[None]


def solution(mesh):
    return jax.shard_map(
        per_device,
        mesh=mesh,
        in_specs=(
            P("section", "seq", None),
            P("section", "seq", None),
            P("section", None, None),
            P("section", None, None),
            P("section", None),
            P("section", None),
            P("section", None),
            P("section", None),
            P("section", None),
            P("section", None),
            P("section", None),
        ),
        out_specs=P("section", "seq", None),
        check_vma=False,
    )
```

profile of v0, /device:TPU:0, one launch (start us, length us, event | category | flops | bytes accessed | tf_op | source)
XLA Modules:
  0.0 589.1 jit_solution(6749542105424368072)
XLA Ops:
  8.6 1.7 slice_reduce_fusion.5
  10.2 1.5 fusion.45
  11.8 391.4 %all-gather.3.cloned.1.call-done = bf16[1,2048,4640]{1,2,0:T(8,128)(2,1)} async-done(((bf16[1,128,4640]{1,2,0:T(8,128)(2,1)}), bf16[1,2048,4640]{1,2,0:T(8,128)(2,1)}) %all-gather.3.cloned.1.call-update) | async-done | bytes 19005456 | tf_op jit(solution)/shard_map/all_gather | solution.py:103
  403.1 9.5 %fusion.12 = bf16[256,4640]{0,1:T(8,128)(2,1)S(1)} fusion(bf16[1,2048,4640]{1,2,0:T(8,128)(2,1)} %all-gather.3.cloned.1.call-done, bf16[1,256,2048]{2,1,0:T(8,128)(2,1)} %param.11, f32[2048]{0:T(1024)} %bitcast.93, f32[256]{0:T(256)S(1)} %add_rsqrt_fusion.1), kind=kOutput, calls=%fused_computation.13 | convolution fusion | flops 4868677632 | bytes 22438912 | tf_op jit(solution)/shard_map/dot_general | solution.py:101
  416.5 4.9 collective-permute-start
  422.4 1.8 copy.19
  424.3 1.8 maximum_convert_fusion
  426.2 4.0 divide_multiply_fusion
  431.7 1.8 fusion.53
  433.5 2.5 collective-permute-start.1
  436.0 20.9 %collective-permute-done.2 = f32[32]{0:T(128)S(1)} collective-permute-done((f32[32]{0:T(128)S(1)}, f32[32]{0:T(128)S(1)}, u32[]{:S(2)}, u32[]{:S(2)}) %collective-permute-start.2) | collective-permute-done | bytes 160 | tf_op jit(solution)/shard_map/ppermute | solution.py:17
  458.4 2.1 collective-permute-done.4
  460.6 2.5 select_bitcast_fusion.3
  464.5 19.9 %collective-permute-done.3 = f32[32,128,64]{1,2,0:T(8,128)S(1)} collective-permute-done((f32[32,128,64]{1,2,0:T(8,128)S(1)}, f32[32,128,64]{1,2,0:T(8,128)S(1)}, u32[]{:S(2)}, u32[]{:S(2)}) %collective-permute-start.3) | collective-permute-done | bytes 1048608 | tf_op jit(solution)/shard_map/ppermute | solution.py:17
  485.7 2.9 collective-permute-start.5
  488.6 19.1 %collective-permute-done.6 = f32[32]{0:T(128)S(1)} collective-permute-done((f32[32]{0:T(128)S(1)}, f32[32]{0:T(128)S(1)}, u32[]{:S(2)}, u32[]{:S(2)}) %collective-permute-start.6) | collective-permute-done | bytes 160 | tf_op jit(solution)/shard_map/ppermute | solution.py:17
  507.7 2.9 select_bitcast_fusion.1
  510.6 3.2 collective-permute-start.7
  515.7 39.3 %collective-permute-done.7 = f32[32,128,64]{1,2,0:T(8,128)} collective-permute-done((f32[32,128,64]{1,2,0:T(8,128)}, f32[32,128,64]{1,2,0:T(8,128)}, u32[]{:S(2)}, u32[]{:S(2)}) %collective-permute-start.7) | collective-permute-done | bytes 1048608 | tf_op jit(solution)/shard_map/ppermute | solution.py:17
  556.5 7.4 %multiply_reduce_fusion = f32[256,32,64]{0,2,1:T(8,128)S(1)} fusion(f32[256,32,4]{0,1,2:T(8,128)S(1)} %copy.35, f32[1,32,128,64]{2,3,1,0:T(8,128)S(1)} %select_bitcast_fusion, f32[1,32,128,64]{2,3,1,0:T(8,128)S(1)} %copy-done.6, f32[1,32,128,64]{2,3,1,0:T(8,128)S(1)} %copy-done.5, f32[1,32,128,64]{2,3,1,0:T(8,128)S(1)} %copy-done.4, ...), kind=kOutput, calls=%fused_computation.4 | convolution fusion | flops 3228041216 | bytes 6553600 | tf_op jit(solution)/shard_map/tn,lhnp->tlhp/dot_general | solution.py:70
  564.0 10.1 %fusion.48 = f32[256,32,64]{0,2,1:T(8,128)S(1)} fusion(f32[256,32,64]{0,2,1:T(8,128)S(1)} %multiply_reduce_fusion, f32[256,32,64]{0,2,1:T(8,128)S(1)} %bitcast.84, f32[256,32]{0,1:T(8,128)S(1)} %bitcast.88, f32[256,32]{0,1:T(8,128)S(1)} %copy-done.17, f32[256,256]{1,0:T(8,128)S(1)} %fusion.67, f32[256,32]{0,1:T(8,128)S(1)} %copy-done.10, ...), kind=kOutput, calls=%fused_computation.52 | convolution fusion | flops 1624768512 | bytes 6717568 | tf_op jit(solution)/shard_map/tsh,shp->thp/dot_general | solution.py:43
  574.0 2.0 multiply_reduce_fusion.1
  576.1 2.5 fusion.32
  578.7 2.6 collective-permute-done.8
  (92 shorter events, 17.1 us)
Async XLA Ops:
  6.5 396.6 %all-gather.3.cloned.1.call-start = ((), (), s32[]{:S(2)}) async-start(), calls=%async_computation | async-start | bytes 20193280 | tf_op jit(solution)/shard_map/all_gather | solution.py:103
  403.1 9.8 %copy-start.20 = (f32[1,32]{1,0:T(1,128)S(1)}, f32[1,32]{1,0:T(1,128)}, u32[]{:S(2)}) copy-start(f32[1,32]{1,0:T(1,128)} %param.16) | copy-start | bytes 388
  403.1 9.8 %copy-start.22 = (f32[1,32]{1,0:T(1,128)S(1)}, f32[1,32]{1,0:T(1,128)}, u32[]{:S(2)}) copy-start(f32[1,32]{1,0:T(1,128)} %param.17) | copy-start | bytes 388
  412.7 11.6 %copy-start.3 = (bf16[256,4640]{0,1:T(8,128)(2,1)}, bf16[256,4640]{0,1:T(8,128)(2,1)S(1)}, u32[]{:S(2)}) copy-start(bf16[256,4640]{0,1:T(8,128)(2,1)S(1)} %fusion.12) | copy-start | bytes 7127044
  416.5 5.9 %collective-permute-start = (bf16[3,2304]{1,0:T(4,128)(2,1)}, bf16[3,2304]{1,0:T(4,128)(2,1)}, u32[]{:S(2)}, u32[]{:S(2)}) collective-permute-start(bf16[3,2304]{1,0:T(4,128)(2,1)} %copy.18), channel_id=1, source_target_pairs={{0,1},{1,2},{2,3},{3,4},{4,5},{5,6},{6,7},{7,8},{8,9},{9,10},{10,1... | collective-permute-start | bytes 41480 | tf_op jit(solution)/shard_map/ppermute | solution.py:23
  433.5 27.1 %collective-permute-start.1 = (f32[32,128,64]{1,2,0:T(8,128)S(1)}, f32[32,128,64]{1,2,0:T(8,128)}, u32[]{:S(2)}, u32[]{:S(2)}) collective-permute-start(f32[32,128,64]{1,2,0:T(8,128)S(1)} %fusion.53), channel_id=1, source_target_pairs={{0,1},{1,0},{2,3},{3,2},{4,5},{5,4},{6,7},{7,6},{8,9},{9,8},{10,11... | collective-permute-start | bytes 3145736 | tf_op jit(solution)/shard_map/ppermute | solution.py:17
  435.9 21.0 %collective-permute-start.2 = (f32[32]{0:T(128)S(1)}, f32[32]{0:T(128)S(1)}, u32[]{:S(2)}, u32[]{:S(2)}) collective-permute-start(f32[32]{0:T(128)S(1)} %copy-done.19), channel_id=1, source_target_pairs={{0,1},{1,0},{2,3},{3,2},{4,5},{5,4},{6,7},{7,6},{8,9},{9,8},{10,11... | collective-permute-start | bytes 392 | tf_op jit(solution)/shard_map/ppermute | solution.py:17
  457.0 3.6 collective-permute-start.4
  463.0 21.3 %collective-permute-start.3 = (f32[32,128,64]{1,2,0:T(8,128)S(1)}, f32[32,128,64]{1,2,0:T(8,128)S(1)}, u32[]{:S(2)}, u32[]{:S(2)}) collective-permute-start(f32[32,128,64]{1,2,0:T(8,128)S(1)} %get-tuple-element.20), channel_id=1, source_target_pairs={{0,2},{2,0},{1,3},{3,1},{4,6},{6,4},{5,7},{7,5},{8,10},{10,8},{9,1... | collective-permute-start | bytes 3145736 | tf_op jit(solution)/shard_map/ppermute | solution.py:17
  485.7 28.2 %copy-start.21 = (f32[1,256]{1,0:T(1,128)S(1)}, f32[1,256]{1,0:T(1,128)}, u32[]{:S(2)}) copy-start(f32[1,256]{1,0:T(1,128)} %param.19) | copy-start | bytes 3076
  485.7 22.0 %collective-permute-start.5 = (f32[32,128,64]{1,2,0:T(8,128)S(1)}, f32[32,128,64]{1,2,0:T(8,128)}, u32[]{:S(2)}, u32[]{:S(2)}) collective-permute-start(f32[32,128,64]{1,2,0:T(8,128)S(1)} %get-tuple-element.22), channel_id=1, source_target_pairs={{0,4},{4,0},{1,5},{5,1},{2,6},{6,2},{3,7},{7,3},{8,12},{12,8},{9,1... | collective-permute-start | bytes 3145736 | tf_op jit(solution)/shard_map/ppermute | solution.py:17
  488.6 19.1 %collective-permute-start.6 = (f32[32]{0:T(128)S(1)}, f32[32]{0:T(128)S(1)}, u32[]{:S(2)}, u32[]{:S(2)}) collective-permute-start(f32[32]{0:T(128)S(1)} %get-tuple-element.29), channel_id=1, source_target_pairs={{0,4},{4,0},{1,5},{5,1},{2,6},{6,2},{3,7},{7,3},{8,12},{12,8},{9,1... | collective-permute-start | bytes 392 | tf_op jit(solution)/shard_map/ppermute | solution.py:17
  507.7 7.5 %copy-start.8 = (f32[256,32]{0,1:T(8,128)S(1)}, f32[256,32]{0,1:T(8,128)}, u32[]{:S(2)}) copy-start(f32[256,32]{0,1:T(8,128)} %get-tuple-element.26) | copy-start | bytes 98308
  510.6 45.8 %copy-start.4 = (f32[1,32,128,64]{2,3,1,0:T(8,128)S(1)}, f32[1,32,128,64]{2,3,1,0:T(8,128)}, u32[]{:S(2)}) copy-start(f32[1,32,128,64]{2,3,1,0:T(8,128)} %get-tuple-element.19) | copy-start | bytes 3145732
  510.6 44.4 %collective-permute-start.7 = (f32[32,128,64]{1,2,0:T(8,128)}, f32[32,128,64]{1,2,0:T(8,128)}, u32[]{:S(2)}, u32[]{:S(2)}) collective-permute-start(f32[32,128,64]{1,2,0:T(8,128)} %get-tuple-element.24), channel_id=1, source_target_pairs={{0,8},{8,0},{1,9},{9,1},{2,10},{10,2},{3,11},{11,3},{4,12},{12,4},... | collective-permute-start | bytes 3145736 | tf_op jit(solution)/shard_map/ppermute | solution.py:17
  513.9 42.6 %copy-start.5 = (f32[1,32,128,64]{2,3,1,0:T(8,128)S(1)}, f32[1,32,128,64]{2,3,1,0:T(8,128)}, u32[]{:S(2)}) copy-start(f32[1,32,128,64]{2,3,1,0:T(8,128)} %get-tuple-element.21) | copy-start | bytes 3145732
  513.9 42.6 %copy-start.6 = (f32[1,32,128,64]{2,3,1,0:T(8,128)S(1)}, f32[1,32,128,64]{2,3,1,0:T(8,128)}, u32[]{:S(2)}) copy-start(f32[1,32,128,64]{2,3,1,0:T(8,128)} %get-tuple-element.23) | copy-start | bytes 3145732
  556.5 7.4 %copy-start.1 = (f32[256,2048]{0,1:T(8,128)S(1)}, f32[256,2048]{0,1:T(8,128)}, u32[]{:S(2)}) copy-start(f32[256,2048]{0,1:T(8,128)} %copy-done) | copy-start | bytes 6291460
  556.5 7.4 %copy-start.10 = (f32[256,32]{0,1:T(8,128)S(1)}, f32[256,32]{0,1:T(8,128)}, u32[]{:S(2)}) copy-start(f32[256,32]{0,1:T(8,128)} %copy-done.9) | copy-start | bytes 98308
  556.5 7.4 %copy-start.17 = (f32[256,32]{0,1:T(8,128)S(1)}, f32[256,32]{0,1:T(8,128)}, u32[]{:S(2)}) copy-start(f32[256,32]{0,1:T(8,128)} %get-tuple-element.17) | copy-start | bytes 98308
  556.5 7.4 %copy-start.23 = (f32[1,32]{1,0:T(1,128)S(1)}, f32[1,32]{1,0:T(1,128)}, u32[]{:S(2)}) copy-start(f32[1,32]{1,0:T(1,128)} %param.18) | copy-start | bytes 388
  563.9 12.2 %slice-start = ((s8[8388608]{0:T(1024)(128)(4,1)}), s8[4194304]{0:T(1024)(128)(4,1)S(1)}, s32[]{:S(2)}) async-start(s8[8388608]{0:T(1024)(128)(4,1)} %bitcast.81), calls=%async_computation.1 | async-start | bytes 8388608
  563.9 12.2 %slice-start.1 = ((s8[8388608]{0:T(1024)(128)(4,1)}), s8[4194304]{0:T(1024)(128)(4,1)S(1)}, s32[]{:S(2)}) async-start(s8[8388608]{0:T(1024)(128)(4,1)} %bitcast.81), calls=%async_computation.2 | async-start | bytes 8388608
  578.6 2.7 collective-permute-start.8
  (12 other events, 28.4 us)
Sparse Core Ops, SparseCore 0:
  8.8 394.2 all-gather.2
where the time goes:
time: 590 us; the launch traced here: 589 us
  waiting for transfers between devices  496 us (84%)
  matrix products  31.6 us (5%)
  other arithmetic  22.6 us (4%)
  starting transfers between devices  16.6 us (3%)
  between operations  13.8 us (2%)
  local copies, waits for them, and re-layouts  8.16 us (1%)
    all_gather x1, waiting for transfers between devices, per_device(): lax.all_gather(in_proj[0], 'seq', axis=0, tiled=True)  391 us
    ppermute x7, waiting for transfers between devices, swapped(): return lax.ppermute(block, axis, route)  101 us
  transfers between devices with their start and end apart: 10, of which 8 were waited for; matrix products, arithmetic and copies ran while one was open for 1% of the time, Pallas kernels for 0%

commit v1 on v0

v1 whole, which is shorter than its diff:
```python
import functools

import jax
import jax.numpy as jnp
from jax import lax
from jax.experimental import pallas as pl
from jax.experimental.pallas import tpu as pltpu
from jax.sharding import PartitionSpec as P

EPS = 1e-05
MESH = pl.DeviceIdType.MESH
f32 = jnp.float32
bf16 = jnp.bfloat16


def remote(src, dst, send, recv, seq):
    return pltpu.make_async_remote_copy(
        src_ref=src,
        dst_ref=dst,
        send_sem=send,
        recv_sem=recv,
        device_id={"seq": seq},
        device_id_type=MESH,
    )


def greet(seq):
    pl.semaphore_signal(
        pltpu.get_barrier_semaphore(), inc=1, device_id={"seq": seq}, device_id_type=MESH
    )


def gather_kernel(
    group, n, u_ref, w_ref, u_all, w_all, u_send, u_recv, w_send, up_send, down_send, w_recv, own_sem
):
    me = lax.axis_index("seq")
    outer = me // group
    inner = lax.rem(me, group)
    outers = n // group
    base = outer * group
    has_up = outer < outers - 1
    has_down = outer > 0
    barrier = pltpu.get_barrier_semaphore()
    for step in range(1, group):
        greet(base + lax.rem(inner + step, group))

    @pl.when(has_up)
    def _():
        greet(me + group)

    @pl.when(has_down)
    def _():
        greet(me - group)

    pl.semaphore_wait(
        barrier, group - 1 + has_up.astype(jnp.int32) + has_down.astype(jnp.int32)
    )

    own_w = pltpu.make_async_copy(w_ref.at[inner], w_all.at[me], own_sem.at[0])
    own_w.start()
    own_u = pltpu.make_async_copy(u_ref, u_all.at[inner], own_sem.at[1])
    own_u.start()

    def up(src, piece):
        return remote(src, w_all.at[piece], up_send.at[piece], w_recv.at[piece], me + group)

    def down(src, piece):
        return remote(src, w_all.at[piece], down_send.at[piece], w_recv.at[piece], me - group)

    def arrived(piece):
        remote(w_all.at[piece], w_all.at[piece], w_send.at[0], w_recv.at[piece], me).wait_recv()

    sends = []
    for step in range(1, group):
        peer = lax.rem(inner + step, group)
        copy = remote(w_ref.at[peer], w_all.at[me], w_send.at[step], w_recv.at[me], base + peer)
        copy.start()
        sends.append(copy)

    @pl.when(has_up)
    def _():
        up(w_ref.at[inner], me).start()

    @pl.when(has_down)
    def _():
        down(w_ref.at[inner], me).start()

    for step in range(1, group):
        peer = lax.rem(inner + step, group)
        copy = remote(u_ref, u_all.at[inner], u_send.at[step], u_recv.at[inner], base + peer)
        copy.start()
        sends.append(copy)

    for step in range(1, group):
        piece = base + lax.rem(inner + step, group)
        arrived(piece)

        @pl.when(has_up)
        def _():
            up(w_all.at[piece], piece).start()

        @pl.when(has_down)
        def _():
            down(w_all.at[piece], piece).start()

    def relay(distance, carry):
        for step in range(group):
            slot = lax.rem(inner + step, group)

            @pl.when(outer - distance >= 0)
            def _():
                piece = (outer - distance) * group + slot
                arrived(piece)

                @pl.when(has_up)
                def _():
                    up(w_all.at[piece], piece).start()

            @pl.when(outer + distance < outers)
            def _():
                piece = (outer + distance) * group + slot
                arrived(piece)

                @pl.when(has_down)
                def _():
                    down(w_all.at[piece], piece).start()

        return carry

    lax.fori_loop(1, outers, relay, 0)

    def drain(piece, carry):
        source = piece // group

        @pl.when(jnp.logical_and(has_up, source <= outer))
        def _():
            up(w_all.at[piece], piece).wait_send()

        @pl.when(jnp.logical_and(has_down, source >= outer))
        def _():
            down(w_all.at[piece], piece).wait_send()

        return carry

    lax.fori_loop(0, n, drain, 0)
    for copy in sends:
        copy.wait_send()
    for step in range(1, group):
        peer = lax.rem(inner + step, group)
        remote(u_ref, u_all.at[peer], u_send.at[0], u_recv.at[peer], me).wait_recv()
    own_w.wait()
    own_u.wait()


def gathered(u, w_parts, n):
    group = w_parts.shape[0]
    dma = pltpu.SemaphoreType.DMA
    return pl.pallas_call(
        functools.partial(gather_kernel, group, n),
        out_shape=(
            jax.ShapeDtypeStruct((group,) + u.shape, u.dtype),
            jax.ShapeDtypeStruct((n,) + w_parts.shape[1:], w_parts.dtype),
        ),
        in_specs=[pl.BlockSpec(memory_space=pltpu.VMEM)] * 2,
        out_specs=[pl.BlockSpec(memory_space=pl.ANY)] * 2,
        scratch_shapes=[
            dma((group,)),
            dma((group,)),
            dma((group,)),
            dma((n,)),
            dma((n,)),
            dma((n,)),
            dma((2,)),
        ],
        compiler_params=pltpu.CompilerParams(collective_id=0, has_side_effects=True),
    )(u, w_parts)


def exchange_kernel(group, x_ref, out_ref, send_sem, recv_sem, own_sem):
    me = lax.axis_index("seq")
    inner = lax.rem(me, group)
    base = me - inner
    for step in range(1, group):
        greet(base + lax.rem(inner + step, group))
    pl.semaphore_wait(pltpu.get_barrier_semaphore(), group - 1)
    sends = []
    for step in range(1, group):
        peer = lax.rem(inner + step, group)
        copy = remote(
            x_ref.at[peer], out_ref.at[inner], send_sem.at[step], recv_sem.at[inner], base + peer
        )
        copy.start()
        sends.append(copy)
    own = pltpu.make_async_copy(x_ref.at[inner], out_ref.at[inner], own_sem)
    own.start()
    own.wait()
    for step in range(1, group):
        peer = lax.rem(inner + step, group)
        remote(x_ref.at[peer], out_ref.at[peer], send_sem.at[0], recv_sem.at[peer], me).wait_recv()
    for copy in sends:
        copy.wait_send()


def exchanged(x):
    group = x.shape[0]
    dma = pltpu.SemaphoreType.DMA
    return pl.pallas_call(
        functools.partial(exchange_kernel, group),
        out_shape=jax.ShapeDtypeStruct(x.shape, x.dtype),
        in_specs=[pl.BlockSpec(memory_space=pltpu.VMEM)],
        out_specs=pl.BlockSpec(memory_space=pltpu.VMEM),
        scratch_shapes=[dma((group,)), dma((group,)), dma],
        compiler_params=pltpu.CompilerParams(collective_id=1, has_side_effects=True),
    )(x)


def swapped(block, axis, apart):
    count = lax.axis_size(axis)
    route = []
    for low in range(count):
        high = low | 1 << apart
        if high != low and high < count:
            route += [(low, high), (high, low)]
    return lax.ppermute(block, axis, route)


def from_behind(block, axis, distance):
    devices = range(lax.axis_size(axis))
    route = [(i - distance, i) for i in devices if i - distance in devices]
    return lax.ppermute(block, axis, route)


def passed_along(value, axis, steps):
    count = lax.axis_size(axis)
    pairs = [(source, (source + steps) % count) for source in range(count)]
    return lax.ppermute(value, axis, pairs)


def per_device(
    acts,
    in_proj,
    out_proj,
    conv_weight,
    conv_bias,
    dt_bias,
    decay_rate,
    skip_gain,
    level_bias,
    norm_gain,
    gate_gain,
):
    n = lax.axis_size("seq")
    group = min(4, n)
    bits = group.bit_length() - 1
    position = lax.axis_index("seq")
    inner_at = lax.rem(position, group)
    hidden = acts[0].astype(f32)
    length = hidden.shape[0]
    inner = gate_gain.shape[1]
    heads = dt_bias.shape[1]
    head_size = inner // heads
    chans = conv_weight.shape[2]
    state = (chans - inner) // 2
    taps = conv_weight.shape[1]
    margin = taps - 1
    levels_all = level_bias.shape[1] // heads
    levels_used = n.bit_length() - 1
    wide = inner // group
    hs = heads // group
    tokens = group * length

    w = in_proj[0]
    rows = w.shape[0]

    def cut(lo, count):
        part = w[:, lo : lo + count].reshape(rows, group, count // group)
        return jnp.swapaxes(part, 0, 1)

    shared = jnp.broadcast_to(w[:, inner:chans][None], (group, rows, 2 * state))
    tail = hs + hs * levels_all
    used = 2 * wide + 2 * state + tail
    padded = -(-used // 128) * 128
    w_parts = jnp.concatenate(
        [
            cut(0, inner),
            shared,
            cut(chans, inner),
            cut(chans + inner, heads),
            cut(chans + inner + heads, heads * levels_all),
            jnp.zeros((group, rows, padded - used), w.dtype),
        ],
        axis=2,
    )
    u = (
        hidden * lax.rsqrt(jnp.mean(hidden * hidden, axis=1, keepdims=True) + EPS) * norm_gain[0]
    ).astype(bf16)
    u_all, w_all = gathered(u, w_parts, n)
    p = jnp.dot(
        u_all.reshape(tokens, -1), w_all.reshape(-1, padded), preferred_element_type=f32
    ).astype(bf16)

    def mine(vector, count):
        return lax.dynamic_slice_in_dim(vector, inner_at * count, count, axis=-1)

    mixed_ch = wide + 2 * state
    own_rows = p[:, :mixed_ch]
    earlier = from_behind(own_rows[tokens - margin :], "seq", group)
    taps_w = jnp.concatenate([mine(conv_weight[0][:, :inner], wide), conv_weight[0][:, inner:]], 1)
    taps_b = jnp.concatenate([mine(conv_bias[0][:inner], wide), conv_bias[0][inner:]], 0)
    conv_in = jnp.concatenate([earlier, own_rows], axis=0).astype(f32)
    mixed = taps_b + jnp.zeros((tokens, mixed_ch), f32)
    for offset in range(taps):
        mixed = mixed + taps_w[offset] * conv_in[offset : offset + tokens]
    mixed = jax.nn.silu(mixed)
    values = mixed[:, :wide].reshape(group, length, hs, head_size)
    b_mat = mixed[:, wide : wide + state].reshape(group, length, state).astype(bf16)
    c_mat = mixed[:, wide + state :].reshape(group, length, state).astype(bf16)
    z_gate = p[:, mixed_ch : mixed_ch + wide].astype(f32)
    at = mixed_ch + wide
    steps = jax.nn.softplus(p[:, at : at + hs].astype(f32) + mine(dt_bias[0], hs))
    steps = steps.reshape(group, length, hs)
    lam = jax.nn.softplus(
        p[:, at + hs : at + tail].astype(f32) + mine(level_bias[0], hs * levels_all)
    ).reshape(group, length, hs, levels_all)
    cum = jnp.cumsum(-steps * mine(decay_rate[0], hs), axis=1)
    ends = cum[:, -1]

    scores = jnp.einsum("btn,bsn->bts", c_mat, b_mat, preferred_element_type=f32)
    cum_t = jnp.swapaxes(cum, 1, 2)
    steps_t = jnp.swapaxes(steps, 1, 2)
    lam0_t = jnp.swapaxes(lam[..., 0], 1, 2)
    row_ids = lax.broadcasted_iota(jnp.int32, (length, length), 0)
    col_ids = lax.broadcasted_iota(jnp.int32, (length, length), 1)
    causal = (col_ids <= row_ids)[None, None]
    differ = cum_t[:, :, :, None] - cum_t[:, :, None, :]
    decays = jnp.exp(jnp.where(causal, differ, -jnp.inf))
    weights = decays * scores[:, None] * (steps_t[:, :, None, :] * lam0_t[:, :, :, None])
    x_bf = values.astype(bf16)
    y = jnp.einsum("bhts,bshp->bthp", weights.astype(bf16), x_bf, preferred_element_type=f32)

    tails = jnp.exp(ends[:, None] - cum) * steps
    states = jnp.einsum(
        "bsn,bshp->bhnp", b_mat, (values * tails[..., None]).astype(bf16), preferred_element_type=f32
    )

    def faded(log, block):
        return jnp.exp(log)[..., None, None] * block

    buckets = [[] for _ in range(group)]
    summed = [states[b] for b in range(group)]
    logs = [ends[b] for b in range(group)]
    before = [jnp.zeros_like(ends[0]) for _ in range(group)]
    for bit in range(bits):
        half = 1 << bit
        merged, merged_logs = [], []
        for g in range(len(summed) // 2):
            low, high = summed[2 * g], summed[2 * g + 1]
            for b in range(2 * g * half, 2 * g * half + half):
                buckets[b].append(None)
            for b in range(2 * g * half + half, 2 * (g + 1) * half):
                buckets[b].append(faded(before[b], low))
                before[b] = before[b] + logs[2 * g]
            merged.append(faded(logs[2 * g + 1], low) + high)
            merged_logs.append(logs[2 * g] + logs[2 * g + 1])
        summed, logs = merged, merged_logs
    block_state, block_log = summed[0], logs[0]
    before_log = jnp.zeros_like(block_log)
    for bit in range(bits, levels_used):
        other_log, other_state = swapped((block_log, block_state), "seq", bit)
        upper = position >> bit & 1 == 1
        bucket = jnp.where(upper, faded(before_log, other_state), 0.0)
        for b in range(group):
            buckets[b].append(faded(before[b], bucket))
        merged_upper = faded(block_log, other_state) + block_state
        merged_lower = faded(other_log, block_state) + other_state
        block_state = jnp.where(upper, merged_upper, merged_lower)
        before_log = jnp.where(upper, before_log + other_log, before_log)
        block_log = block_log + other_log

    zero = jnp.zeros_like(states[0])
    stacked = jnp.stack(
        [jnp.stack([zero if s is None else s for s in buckets[b]]) for b in range(group)]
    )
    reads = jnp.einsum(
        "btn,blhnp->btlhp", c_mat, stacked.astype(bf16), preferred_element_type=f32
    )
    scale = lam[..., 1 : levels_used + 1] * jnp.exp(cum)[..., None]
    for level in range(levels_used):
        y = y + scale[..., level][..., None] * reads[:, :, level]
    y = y + mine(skip_gain[0], hs)[:, None] * values
    gated = y.reshape(tokens, wide) * jax.nn.silu(z_gate)

    own = exchanged(gated.astype(bf16).reshape(group, length, wide))
    own = jnp.swapaxes(own, 0, 1).reshape(length, inner).astype(f32)
    normed = (
        own * lax.rsqrt(jnp.mean(own * own, axis=1, keepdims=True) + EPS) * gate_gain[0]
    ).astype(bf16)
    result = (hidden + jnp.dot(normed, out_proj[0], preferred_element_type=f32)).astype(bf16)
    moved = passed_along(result, "section", 1)
    return moved[None]


def solution(mesh):
    return jax.shard_map(
        per_device,
        mesh=mesh,
        in_specs=(
            P("section", "seq", None),
            P("section", "seq", None),
            P("section", None, None),
            P("section", None, None),
            P("section", None),
            P("section", None),
            P("section", None),
            P("section", None),
            P("section", None),
            P("section", None),
            P("section", None),
        ),
        out_specs=P("section", "seq", None),
        check_vma=False,
    )
```

time: 590 us -> 226 us (0.38)
  waiting for transfers between devices: 496 us -> 13.6 us
  Pallas kernels: 0 us -> 124 us
  local copies, waits for them, and re-layouts: 8.16 us -> 32.1 us
  between operations: 13.8 us -> 0.74 us
  starting transfers between devices: 16.6 us -> 5.48 us
  matrix products: 31.6 us -> 22.3 us
    all_gather x1 -> x0, waiting for transfers between devices: 391 us -> none  [per_device(): lax.all_gather(in_proj[0], 'seq', axis=0, tiled=True)]
    pallas_call x0 -> x2, Pallas kernels: none -> 124 us  [the longest x1 110 us: gathered(): pl.pallas_call(functools.partial(gather_kernel, group, n), out_shape=(jax...]
    ppermute x7 -> x3, waiting for transfers between devices: 101 us -> 11 us  [swapped(): return lax.ppermute(block, axis, route)]
    dot_general x6, matrix products: 31.6 us -> 22.3 us  [the longest x1 9.7 us: per_device(): jnp.dot(u_all.reshape(tokens, -1), w_all.reshape(-1, padded), preferred_e...]
    ppermute x7 -> x3, starting transfers between devices: 11.7 us -> 3.95 us  [swapped(): return lax.ppermute(block, axis, route)]
    slice x8 -> x24, local copies, waits for them, and re-layouts: 3.31 us -> 9.43 us  [the longest x5 2.46 us: per_device(): y = y + scale[..., level][..., None] * reads[:, :, level]]
  transfers between devices with their start and end apart: 10 -> 5, of which waited for: 8 -> 3; matrix products, arithmetic and copies ran while one was open for 1% -> 11% of each run, Pallas kernels for 0% -> 0%
where the time goes in v1:
time: 226 us; the launch traced here: 225 us
  Pallas kernels  124 us (55%)
  local copies, waits for them, and re-layouts  32.1 us (14%)
  other arithmetic  26.1 us (12%)
  matrix products  22.3 us (10%)
  waiting for transfers between devices  13.6 us (6%)
  starting transfers between devices  5.48 us (2%)
    pallas_call x1, Pallas kernels, gathered(): pl.pallas_call(functools.partial(gather_kernel, group, n), out_shape=(jax...  110 us
    pallas_call x1, Pallas kernels, exchanged(): pl.pallas_call(functools.partial(exchange_kernel, group), out_shape=jax.S...  14.7 us
    ppermute x3, waiting for transfers between devices, swapped(): return lax.ppermute(block, axis, route)  11 us
    dot_general x1, matrix products, per_device(): jnp.dot(u_all.reshape(tokens, -1), w_all.reshape(-1, padded), preferred_e...  9.7 us
    another operation x5, other arithmetic  7.09 us
    unnamed x83, local copies, waits for them, and re-layouts  6.24 us
    dot_general x1, matrix products, per_device(): jnp.dot(normed, out_proj[0], preferred_element_type=f32)  5.74 us
  transfers between devices with their start and end apart: 5, of which 3 were waited for; matrix products, arithmetic and copies ran while one was open for 11% of the time, Pallas kernels for 0%

profile of v1, /device:TPU:0, one launch (start us, length us, event | category | flops | bytes accessed | tf_op | source)
XLA Modules:
  0.0 224.7 jit_solution(10563850187221846576)
XLA Ops:
  0.0 1.4 fusion.83
  5.5 1.9 concatenate.14.w_ref
  7.4 109.6 %shard_map.109 = (bf16[4,256,2048]{2,1,0:T(8,128)(2,1)}, bf16[16,128,1408]{2,1,0:T(8,128)(2,1)}) custom-call(bf16[256,2048]{1,0:T(8,128)(2,1)} %fusion.28.u_ref, bf16[4,128,1408]{2,1,0:T(8,128)(2,1)} %concatenate.14.w_ref), custom_call_target="tpu_custom_call" | custom-call | tf_op jit(solution)/shard_map/pallas_call | solution.py:158
  117.0 9.7 %convolution_convert_fusion = bf16[1024,1408]{0,1:T(8,128)(2,1)S(1)} fusion(bf16[1024,2048]{1,0:T(8,128)(2,1)} %bitcast.221, bf16[2048,1408]{1,0:T(8,128)(2,1)} %bitcast.220), kind=kOutput, calls=%fused_computation.11 | convolution fusion | flops 5907021824 | bytes 12845056 | tf_op jit(solution)/shard_map/dot_general | solution.py:298
  126.8 1.6 copy-done.3
  128.5 1.5 collective-permute-start
  130.9 2.3 %reduce-window.6 = f32[4,8,2,128]{3,1,2,0:T(8,128)S(1)} reduce-window(f32[4,8,2,128]{3,1,2,0:T(8,128)S(1)} %multiply_bitcast_fusion, f32[]{:T(128)} %constant.23.clone.1), window={size=1x1x1x128 pad=0_0x0_0x0_0x127_0}, to_apply=%region_1.2 | reduce-window | flops 1040384 | bytes 65540 | tf_op jit(solution)/shard_map/reduce-window
  135.5 1.6 collective-permute-start.2
  148.1 1.4 reduce.25
  153.6 3.3 %fusion.80 = (bf16[1024,768]{0,1:T(8,128)(2,1)S(1)}, f32[1024,768]{0,1:T(8,128)S(1)}) fusion(f32[1027,768]{0,1:T(8,128)S(1)} %maximum_convert_fusion, f32[768]{0:T(1024)S(1)} %get-tuple-element.16, f32[768]{0:T(1024)S(1)} %get-tuple-element.17, f32[768]{0:T(1024)S(1)} %get-tuple-element.15, f32[768]{0:T(1024)S(1)} %get-tuple-element.14, ...), kind=kLoop, calls=%fused_computation.160 | loop fusion | flops 10223616 | bytes 17316864 | tf_op jit(solution)/shard_map/convert.33
  157.7 1.5 slice.219
  159.2 2.4 %reshape.210 = f32[4,256,8,64]{1,0,3,2:T(4,128)S(1)} reshape(f32[1024,512]{0,1:T(8,128)} %slice.219) | data formatting | bytes 4194304 | tf_op jit(solution)/shard_map/reshape | solution.py:315
  161.6 1.8 convert_element_type.71
  167.6 3.8 %collective-permute-done.1 = f32[8,128,64]{1,2,0:T(8,128)S(1)} collective-permute-done((f32[8,128,64]{1,2,0:T(8,128)S(1)}, f32[8,128,64]{1,2,0:T(8,128)S(1)}, u32[]{:S(2)}, u32[]{:S(2)}) %collective-permute-start.1) | collective-permute-done | bytes 262176 | tf_op jit(solution)/shard_map/ppermute | solution.py:224
  173.2 1.9 collective-permute-start.3
  176.8 7.1 %collective-permute-done.3 = f32[8,128,64]{1,2,0:T(8,128)} collective-permute-done((f32[8,128,64]{1,2,0:T(8,128)}, f32[8,128,64]{1,2,0:T(8,128)}, u32[]{:S(2)}, u32[]{:S(2)}) %collective-permute-start.3) | collective-permute-done | bytes 262176 | tf_op jit(solution)/shard_map/ppermute | solution.py:224
  187.9 3.9 %fusion.31 = f32[4,256,8,64]{1,3,2,0:T(8,128)S(1)} fusion(f32[4,256,4,8,64]{1,4,3,0,2:T(8,128)S(1)} %fusion.38, f32[4,256,8,64]{1,0,3,2:T(4,128)S(1)} %reshape.210, f32[4,8,256]{2,1,0:T(8,128)S(1)} %bitcast.212, f32[4,8,256]{2,1,0:T(8,128)S(1)} %bitcast.208, f32[4,256,256]{2,1,0:T(8,128)S(1)} %copy-done.8, f32[4,8,256]{2,1,0:T(8,128)S(1)} %copy-done.19, ...), kind=kOutput, calls=%fused_computation.42 | convolution fusion | flops 286785536 | bytes 16056832 | tf_op jit(solution)/shard_map/bhts,bshp->bthp/dot_general | solution.py:339
  191.7 1.4 copy.116
  193.6 1.3 copy-done.4
  196.9 14.7 %shard_map.110 = bf16[4,256,512]{2,1,0:T(8,128)(2,1)} custom-call(bf16[4,256,512]{2,1,0:T(8,128)(2,1)} %bitcast.191), custom_call_target="tpu_custom_call" | custom-call | tf_op jit(solution)/shard_map/pallas_call | solution.py:207
  211.6 1.5 fusion.23
  213.1 1.5 fusion.41
  215.2 5.7 %fusion.16 = bf16[256,2048]{1,0:T(8,128)(2,1)S(1)} fusion(bf16[256,2048]{0,1:T(8,128)(2,1)S(1)} %bitcast.190, bf16[1,2048,2048]{2,1,0:T(8,128)(2,1)} %param.13, bf16[1,256,2048]{2,1,0:T(8,128)(2,1)S(1)} %copy-done.2), kind=kOutput, calls=%fused_computation.28 | convolution fusion | flops 2149056512 | bytes 11534336 | tf_op jit(solution)/shard_map/dot_general | solution.py:398
  221.1 2.6 %collective-permute-done.4 = bf16[256,2048]{1,0:T(8,128)(2,1)S(1)} collective-permute-done((bf16[256,2048]{1,0:T(8,128)(2,1)S(1)}, bf16[256,2048]{1,0:T(8,128)(2,1)S(1)}, u32[]{:S(2)}, u32[]{:S(2)}) %collective-permute-start.4) | collective-permute-done | bytes 1048608 | tf_op jit(solution)/shard_map/ppermute | solution.py:236
  (163 shorter events, 38.5 us)
Async XLA Ops:
  0.0 141.0 %copy-start = (f32[1,256]{1,0:T(1,128)S(1)}, f32[1,256]{1,0:T(1,128)}, u32[]{:S(2)}) copy-start(f32[1,256]{1,0:T(1,128)} %param.19) | copy-start | bytes 3076
  117.0 12.9 %copy-start.36 = (f32[1,32]{1,0:T(1,128)S(1)}, f32[1,32]{1,0:T(1,128)}, u32[]{:S(2)}) copy-start(f32[1,32]{1,0:T(1,128)} %param.16) | copy-start | bytes 388
  117.0 12.9 %copy-start.37 = (f32[1,32]{1,0:T(1,128)S(1)}, f32[1,32]{1,0:T(1,128)}, u32[]{:S(2)}) copy-start(f32[1,32]{1,0:T(1,128)} %param.17) | copy-start | bytes 388
  128.3 8.8 %copy-start.18 = (f32[1,4,2304]{2,1,0:T(4,128)S(1)}, f32[1,4,2304]{2,1,0:T(4,128)}, u32[]{:S(2)}) copy-start(f32[1,4,2304]{2,1,0:T(4,128)} %param.14) | copy-start | bytes 110596
  128.3 8.8 %copy-start.25 = (f32[1,2304]{1,0:T(1,128)S(1)}, f32[1,2304]{1,0:T(1,128)}, u32[]{:S(2)}) copy-start(f32[1,2304]{1,0:T(1,128)} %param.15) | copy-start | bytes 27652
  128.3 11.4 %slice-start.1 = ((f32[1,2304]{1,0:T(1,128)}), f32[1,2048]{1,0:T(1,128)S(1)}, s32[]{:S(2)}) async-start(f32[1,2304]{1,0:T(1,128)} %param.15), calls=%async_computation.1 | async-start | bytes 16384 | tf_op jit(solution)/shard_map/slice | solution.py:309
  128.5 24.4 %collective-permute-start = (bf16[3,768]{0,1:T(8,128)(2,1)S(1)}, bf16[3,768]{0,1:T(8,128)(2,1)S(1)}, u32[]{:S(2)}, u32[]{:S(2)}) collective-permute-start(bf16[3,768]{0,1:T(8,128)(2,1)S(1)} %slice.209), channel_id=1, source_target_pairs={{0,4},{1,5},{2,6},{3,7},{4,8},{5,9},{6,10},{7,11},{8,12},{9,13},{1... | collective-permute-start | bytes 13832 | tf_op jit(solution)/shard_map/ppermute | solution.py:230
  130.8 10.2 %copy-start.14 = (f32[1024,8]{0,1:T(8,128)}, f32[1024,8]{0,1:T(8,128)S(1)}, u32[]{:S(2)}) copy-start(f32[1024,8]{0,1:T(8,128)S(1)} %compare_select_fusion.1) | copy-start | bytes 98308
  135.5 17.3 %slice-start = ((bf16[1024,1408]{0,1:T(8,128)(2,1)}), bf16[1024,768]{0,1:T(8,128)(2,1)S(1)}, s32[]{:S(2)}) async-start(bf16[1024,1408]{0,1:T(8,128)(2,1)} %copy-done.3), calls=%async_computation | async-start | bytes 3145728 | tf_op jit(solution)/shard_map/slice | solution.py:306
  135.5 16.1 %collective-permute-start.2 = (f32[8]{0:T(128)}, f32[8]{0:T(128)}, u32[]{:S(2)}, u32[]{:S(2)}) collective-permute-start(f32[8]{0:T(128)} %get-tuple-element.21), channel_id=1, source_target_pairs={{0,4},{4,0},{1,5},{5,1},{2,6},{6,2},{3,7},{7,3},{8,12},{12,8},{9,1... | collective-permute-start | bytes 104 | tf_op jit(solution)/shard_map/ppermute | solution.py:224
  164.8 7.4 %copy-start.30 = (f32[8]{0:T(128)S(1)}, f32[8]{0:T(128)}, u32[]{:S(2)}) copy-start(f32[8]{0:T(128)} %get-tuple-element.9) | copy-start | bytes 100
  164.8 7.3 %copy-start.31 = (f32[8]{0:T(128)S(1)}, f32[8]{0:T(128)}, u32[]{:S(2)}) copy-start(f32[8]{0:T(128)} %get-tuple-element.48) | copy-start | bytes 100
  164.8 7.3 %copy-start.32 = (f32[8]{0:T(128)S(1)}, f32[8]{0:T(128)}, u32[]{:S(2)}) copy-start(f32[8]{0:T(128)} %get-tuple-element.52) | copy-start | bytes 100
  164.8 7.3 %copy-start.33 = (f32[8]{0:T(128)S(1)}, f32[8]{0:T(128)}, u32[]{:S(2)}) copy-start(f32[8]{0:T(128)} %get-tuple-element.20) | copy-start | bytes 100
  164.9 7.3 %copy-start.35 = (f32[8]{0:T(128)S(1)}, f32[8]{0:T(128)}, u32[]{:S(2)}) copy-start(f32[8]{0:T(128)} %get-tuple-element.54) | copy-start | bytes 100
  165.0 6.4 %collective-permute-start.1 = (f32[8,128,64]{1,2,0:T(8,128)S(1)}, f32[8,128,64]{1,2,0:T(8,128)S(1)}, u32[]{:S(2)}, u32[]{:S(2)}) collective-permute-start(f32[8,128,64]{1,2,0:T(8,128)S(1)} %fusion.49), channel_id=1, source_target_pairs={{0,4},{4,0},{1,5},{5,1},{2,6},{6,2},{3,7},{7,3},{8,12},{12,8},{9,1... | collective-permute-start | bytes 786440 | tf_op jit(solution)/shard_map/ppermute | solution.py:224
  173.2 11.8 %copy-start.38 = (bf16[4]{0:T(256)(128)(2,1)S(1)}, bf16[4]{0:T(256)(128)(2,1)}, u32[]{:S(2)}) copy-start(bf16[4]{0:T(256)(128)(2,1)} %pad.16.clone) | copy-start | bytes 28
  173.2 10.7 %collective-permute-start.3 = (f32[8,128,64]{1,2,0:T(8,128)}, f32[8,128,64]{1,2,0:T(8,128)}, u32[]{:S(2)}, u32[]{:S(2)}) collective-permute-start(f32[8,128,64]{1,2,0:T(8,128)} %get-tuple-element.41), channel_id=1, source_target_pairs={{0,8},{8,0},{1,9},{9,1},{2,10},{10,2},{3,11},{11,3},{4,12},{12,4},... | collective-permute-start | bytes 786440 | tf_op jit(solution)/shard_map/ppermute | solution.py:224
  176.7 9.5 %copy-start.10 = (bf16[1,8,128,64]{2,3,1,0:T(8,128)(2,1)S(1)}, bf16[1,8,128,64]{2,3,1,0:T(8,128)(2,1)}, u32[]{:S(2)}) copy-start(bf16[1,8,128,64]{2,3,1,0:T(8,128)(2,1)} %get-tuple-element.38) | copy-start | bytes 393220
  176.7 9.5 %copy-start.11 = (bf16[1,8,128,64]{2,3,1,0:T(8,128)(2,1)S(1)}, bf16[1,8,128,64]{2,3,1,0:T(8,128)(2,1)}, u32[]{:S(2)}) copy-start(bf16[1,8,128,64]{2,3,1,0:T(8,128)(2,1)} %get-tuple-element.39) | copy-start | bytes 393220
  176.7 9.5 %copy-start.12 = (bf16[1,8,128,64]{2,3,1,0:T(8,128)(2,1)S(1)}, bf16[1,8,128,64]{2,3,1,0:T(8,128)(2,1)}, u32[]{:S(2)}) copy-start(bf16[1,8,128,64]{2,3,1,0:T(8,128)(2,1)} %get-tuple-element.30) | copy-start | bytes 393220
  176.7 9.6 %copy-start.13 = (bf16[1,8,128,64]{2,3,1,0:T(8,128)(2,1)S(1)}, bf16[1,8,128,64]{2,3,1,0:T(8,128)(2,1)}, u32[]{:S(2)}) copy-start(bf16[1,8,128,64]{2,3,1,0:T(8,128)(2,1)} %get-tuple-element.32) | copy-start | bytes 393220
  215.2 9.5 %copy-start.1 = (f32[1,256]{1,0:T(1,128)S(1)}, f32[1,256]{1,0:T(1,128)}, u32[]{:S(2)}) copy-start(f32[1,256]{1,0:T(1,128)} %param.19) | copy-start | bytes 3076
  221.0 2.7 %collective-permute-start.4 = (bf16[256,2048]{1,0:T(8,128)(2,1)S(1)}, bf16[256,2048]{1,0:T(8,128)(2,1)S(1)}, u32[]{:S(2)}, u32[]{:S(2)}) collective-permute-start(bf16[256,2048]{1,0:T(8,128)(2,1)S(1)} %fusion.16), channel_id=1, source_target_pairs={{0,16},{16,0},{1,17},{17,1},{2,18},{18,2},{3,19},{19,3},{4,20},{20... | collective-permute-start | bytes 3145736 | tf_op jit(solution)/shard_map/ppermute | solution.py:236
  (23 other events, 37.7 us)

commit v2 on v1

v2 whole, which is shorter than its diff:
```python
import functools

import jax
import jax.numpy as jnp
from jax import lax
from jax.experimental import pallas as pl
from jax.experimental.pallas import tpu as pltpu
from jax.sharding import PartitionSpec as P

EPS = 1e-05
MESH = pl.DeviceIdType.MESH
f32 = jnp.float32
bf16 = jnp.bfloat16


def remote(src, dst, send, recv, seq):
    return pltpu.make_async_remote_copy(
        src_ref=src,
        dst_ref=dst,
        send_sem=send,
        recv_sem=recv,
        device_id={"seq": seq},
        device_id_type=MESH,
    )


def greet(seq):
    pl.semaphore_signal(
        pltpu.get_barrier_semaphore(), inc=1, device_id={"seq": seq}, device_id_type=MESH
    )


def gather_kernel(
    group, n, u_ref, w_ref, p_ref, u_all, w_all, acc, u_send, u_recv, w_send, up_send, down_send, w_recv, own_sem
):
    me = lax.axis_index("seq")
    outer = me // group
    inner = lax.rem(me, group)
    outers = n // group
    base = outer * group
    length = u_ref.shape[1]
    rows = w_ref.shape[1]
    has_up = outer < outers - 1
    has_down = outer > 0
    barrier = pltpu.get_barrier_semaphore()
    for step in range(1, group):
        greet(base + lax.rem(inner + step, group))

    @pl.when(has_up)
    def _():
        greet(me + group)

    @pl.when(has_down)
    def _():
        greet(me - group)

    pl.semaphore_wait(
        barrier, group - 1 + has_up.astype(jnp.int32) + has_down.astype(jnp.int32)
    )

    def w_slot(source, slot):
        return w_all.at[source, pl.ds(pl.multiple_of(slot * rows, rows), rows), :]

    def u_slot(slot):
        return u_all.at[:, slot]

    own_w = pltpu.make_async_copy(w_ref.at[inner], w_slot(outer, inner), own_sem.at[0])
    own_w.start()
    own_u = pltpu.make_async_copy(u_ref, u_slot(inner), own_sem.at[1])
    own_u.start()

    def up(src, source, slot):
        at = source * group + slot
        return remote(src, w_slot(source, slot), up_send.at[at], w_recv.at[at], me + group)

    def down(src, source, slot):
        at = source * group + slot
        return remote(src, w_slot(source, slot), down_send.at[at], w_recv.at[at], me - group)

    def arrived(source, slot):
        piece = w_slot(source, slot)
        remote(piece, piece, w_send.at[0], w_recv.at[source * group + slot], me).wait_recv()

    sends = []
    for step in range(1, group):
        peer = lax.rem(inner + step, group)
        copy = remote(
            w_ref.at[peer], w_slot(outer, inner), w_send.at[step], w_recv.at[me], base + peer
        )
        copy.start()
        sends.append(copy)

    @pl.when(has_up)
    def _():
        up(w_ref.at[inner], outer, inner).start()

    @pl.when(has_down)
    def _():
        down(w_ref.at[inner], outer, inner).start()

    for step in range(1, group):
        slot = lax.rem(inner + step, group)
        arrived(outer, slot)

        @pl.when(has_up)
        def _():
            up(w_slot(outer, slot), outer, slot).start()

        @pl.when(has_down)
        def _():
            down(w_slot(outer, slot), outer, slot).start()

    for step in range(1, group):
        peer = lax.rem(inner + step, group)
        copy = remote(u_ref, u_slot(inner), u_send.at[step], u_recv.at[inner], base + peer)
        copy.start()
        sends.append(copy)

    def multiply(source, block, first=False):
        part = jnp.dot(u_all[source, block], w_all[source], preferred_element_type=f32)
        if first:
            acc[block] = part
        else:
            acc[block] += part

    def multiply_both(distance, block):
        @pl.when(outer - distance >= 0)
        def _():
            multiply(outer - distance, block)

        @pl.when(outer + distance < outers)
        def _():
            multiply(outer + distance, block)

    def relay(distance, block):
        slot = lax.rem(inner + block, group)

        @pl.when(outer - distance >= 0)
        def _():
            arrived(outer - distance, slot)

            @pl.when(has_up)
            def _():
                up(w_slot(outer - distance, slot), outer - distance, slot).start()

        @pl.when(outer + distance < outers)
        def _():
            arrived(outer + distance, slot)

            @pl.when(has_down)
            def _():
                down(w_slot(outer + distance, slot), outer + distance, slot).start()

    def relay_first(block, carry):
        relay(1, block)
        return carry

    if outers > 1:
        lax.fori_loop(0, group, relay_first, 0)
    own_w.wait()
    own_u.wait()
    for step in range(1, group):
        peer = lax.rem(inner + step, group)
        remote(u_slot(peer), u_slot(peer), u_send.at[0], u_recv.at[peer], me).wait_recv()

    def own_work(block, carry):
        multiply(outer, block, True)
        return carry

    lax.fori_loop(0, group, own_work, 0)

    def later(step, carry):
        distance = step // group
        block = lax.rem(step, group)
        relay(distance, block)
        multiply_both(distance - 1, block)
        return carry

    lax.fori_loop(2 * group, outers * group, later, 0)

    def finish(block, carry):
        if outers > 1:
            multiply_both(outers - 1, block)
        p_ref[block] = acc[block].astype(p_ref.dtype)
        return carry

    lax.fori_loop(0, group, finish, 0)

    def drain(at, carry):
        source = at // group
        slot = lax.rem(at, group)

        @pl.when(jnp.logical_and(has_up, source <= outer))
        def _():
            up(w_slot(source, slot), source, slot).wait_send()

        @pl.when(jnp.logical_and(has_down, source >= outer))
        def _():
            down(w_slot(source, slot), source, slot).wait_send()

        return carry

    lax.fori_loop(0, n, drain, 0)
    for copy in sends:
        copy.wait_send()


def gathered(u, w_parts, n):
    group, rows, columns = w_parts.shape
    outers, length, depth = u.shape
    dma = pltpu.SemaphoreType.DMA
    return pl.pallas_call(
        functools.partial(gather_kernel, group, n),
        out_shape=jax.ShapeDtypeStruct((group, length, columns), bf16),
        in_specs=[pl.BlockSpec(memory_space=pltpu.VMEM)] * 2,
        out_specs=pl.BlockSpec(memory_space=pltpu.VMEM),
        scratch_shapes=[
            pltpu.VMEM((outers, group, length, depth), bf16),
            pltpu.VMEM((outers, group * rows, columns), bf16),
            pltpu.VMEM((group, length, columns), f32),
            dma((group,)),
            dma((group,)),
            dma((group,)),
            dma((n,)),
            dma((n,)),
            dma((n,)),
            dma((2,)),
        ],
        compiler_params=pltpu.CompilerParams(
            collective_id=0, has_side_effects=True, vmem_limit_bytes=56 << 20
        ),
    )(u, w_parts)


def selector(lanes, wide, size, first, stride):
    row = lax.broadcasted_iota(jnp.int32, (lanes, wide), 0)
    head = lax.broadcasted_iota(jnp.int32, (lanes, wide), 1) // size
    return jnp.where(row == head * stride + first, 1.0, 0.0).astype(bf16)


def spread(value, pick):
    high = value.astype(bf16)
    low = (value - high.astype(f32)).astype(bf16)
    return jnp.dot(high, pick, preferred_element_type=f32) + jnp.dot(
        low, pick, preferred_element_type=f32
    )


def silu(value):
    return value / (1.0 + jnp.exp(-value))


def softplus(value):
    return jnp.maximum(value, 0.0) + jnp.log1p(jnp.exp(-jnp.abs(value)))


def state_kernel(
    dims, p_ref, halo_ref, taps_ref, bias_ref, small_bias_ref, rate_ref, x_ref, bc_ref, small_ref, cum_ref, state_ref
):
    wide, state, size, taps = dims
    mixed_ch = wide + 2 * state
    length = p_ref.shape[1]
    raw = p_ref[0, :, :mixed_ch].astype(f32)
    ext = jnp.concatenate([halo_ref[0], raw], axis=0)
    first = halo_ref.shape[1] - taps + 1
    mixed = bias_ref[...] + taps_ref[taps - 1 :] * raw
    for k in range(taps - 1):
        mixed = mixed + taps_ref[k : k + 1] * ext[first + k : first + k + length]
    mixed = silu(mixed)
    x = mixed[:, :wide]
    x_ref[0] = x.astype(bf16)
    bc = mixed[:, wide:].astype(bf16)
    bc_ref[0] = bc
    small = softplus(p_ref[0, :, mixed_ch + wide :].astype(f32) + small_bias_ref[...])
    small_ref[0] = small
    rows = lax.broadcasted_iota(jnp.int32, (length, length), 0)
    cols = lax.broadcasted_iota(jnp.int32, (length, length), 1)
    below = jnp.where(cols <= rows, 1.0, 0.0)
    cum = jnp.dot(
        below,
        -small * rate_ref[...],
        precision=lax.Precision.HIGHEST,
        preferred_element_type=f32,
    )
    cum_ref[0] = cum
    tail = jnp.exp(cum[length - 1 :] - cum) * small
    faded = (x * spread(tail, selector(small.shape[1], wide, size, 0, 1))).astype(bf16)
    state_ref[0] = lax.dot_general(
        bc[:, :state], faded, (((0,), (0,)), ((), ())), preferred_element_type=f32
    )


def inside_kernel(dims, levels, x_ref, bc_ref, small_ref, cum_ref, skip_ref, y_ref):
    wide, state, size, _ = dims
    hs = wide // size
    length = x_ref.shape[1]
    lanes = small_ref.shape[2]
    bc = bc_ref[0]
    scores = lax.dot_general(
        bc[:, state:], bc[:, :state], (((1,), (1,)), ((), ())), preferred_element_type=f32
    )
    rows = lax.broadcasted_iota(jnp.int32, (length, length), 0)
    cols = lax.broadcasted_iota(jnp.int32, (length, length), 1)
    causal = cols <= rows
    small = small_ref[0]
    cum = cum_ref[0]
    cum_rows = jnp.transpose(cum)
    x = x_ref[0].astype(f32)
    stepped = (x * spread(small, selector(lanes, wide, size, 0, 1))).astype(bf16)
    parts = []
    for h in range(hs):
        differ = cum[:, h : h + 1] - cum_rows[h : h + 1, :]
        weights = jnp.exp(jnp.where(causal, differ, -1e30)) * scores
        parts.append(
            jnp.dot(
                weights.astype(bf16),
                stepped[:, h * size : (h + 1) * size],
                preferred_element_type=f32,
            )
        )
    y = jnp.concatenate(parts, axis=1)
    own = spread(small, selector(lanes, wide, size, hs, levels))
    y_ref[0] = y * own + skip_ref[...] * x


def outside_kernel(dims, levels, used, y_ref, bc_ref, bucket_ref, small_ref, cum_ref, p_ref, q_ref):
    wide, state, size, _ = dims
    hs = wide // size
    lanes = small_ref.shape[2]
    c = bc_ref[0, :, state:]
    small = small_ref[0]
    total = None
    for level in range(used):
        reads = jnp.dot(c, bucket_ref[0, level], preferred_element_type=f32)
        term = reads * spread(small, selector(lanes, wide, size, hs + level + 1, levels))
        total = term if total is None else total + term
    y = y_ref[0]
    if total is not None:
        y = y + total * spread(jnp.exp(cum_ref[0]), selector(lanes, wide, size, 0, 1))
    at = wide + 2 * state
    q_ref[0] = (y * silu(p_ref[0, :, at : at + wide].astype(f32))).astype(bf16)


def blocked(shape):
    rest = len(shape) - 1
    return pl.BlockSpec((1,) + tuple(shape[1:]), lambda b: (b,) + (0,) * rest)


def whole(shape):
    rest = len(shape)
    return pl.BlockSpec(tuple(shape), lambda b: (0,) * rest)


def per_block(kernel, group, split, fixed, outs, flops):
    order = split + fixed
    specs = [blocked(v.shape) for v in split] + [whole(v.shape) for v in fixed]
    moved = sum(v.size * v.dtype.itemsize for v in order)
    return pl.pallas_call(
        kernel,
        grid=(group,),
        out_shape=outs,
        in_specs=specs,
        out_specs=[blocked(o.shape) for o in outs],
        compiler_params=pltpu.CompilerParams(vmem_limit_bytes=40 << 20),
        cost_estimate=pl.CostEstimate(flops=flops, bytes_accessed=moved, transcendentals=0),
    )(*order)


def exchange_kernel(group, x_ref, out_ref, send_sem, recv_sem, own_sem):
    me = lax.axis_index("seq")
    inner = lax.rem(me, group)
    base = me - inner
    for step in range(1, group):
        greet(base + lax.rem(inner + step, group))
    pl.semaphore_wait(pltpu.get_barrier_semaphore(), group - 1)
    sends = []
    for step in range(1, group):
        peer = lax.rem(inner + step, group)
        copy = remote(
            x_ref.at[peer], out_ref.at[inner], send_sem.at[step], recv_sem.at[inner], base + peer
        )
        copy.start()
        sends.append(copy)
    own = pltpu.make_async_copy(x_ref.at[inner], out_ref.at[inner], own_sem)
    own.start()
    own.wait()
    for step in range(1, group):
        peer = lax.rem(inner + step, group)
        remote(x_ref.at[peer], out_ref.at[peer], send_sem.at[0], recv_sem.at[peer], me).wait_recv()
    for copy in sends:
        copy.wait_send()


def exchanged(x):
    group = x.shape[0]
    dma = pltpu.SemaphoreType.DMA
    return pl.pallas_call(
        functools.partial(exchange_kernel, group),
        out_shape=jax.ShapeDtypeStruct(x.shape, x.dtype),
        in_specs=[pl.BlockSpec(memory_space=pltpu.VMEM)],
        out_specs=pl.BlockSpec(memory_space=pltpu.VMEM),
        scratch_shapes=[dma((group,)), dma((group,)), dma],
        compiler_params=pltpu.CompilerParams(collective_id=1, has_side_effects=True),
    )(x)


def swapped(block, axis, apart):
    count = lax.axis_size(axis)
    route = []
    for low in range(count):
        high = low | 1 << apart
        if high != low and high < count:
            route += [(low, high), (high, low)]
    return lax.ppermute(block, axis, route)


def from_behind(block, axis, distance):
    devices = range(lax.axis_size(axis))
    route = [(i - distance, i) for i in devices if i - distance in devices]
    return lax.ppermute(block, axis, route)


def passed_along(value, axis, steps):
    count = lax.axis_size(axis)
    pairs = [(source, (source + steps) % count) for source in range(count)]
    return lax.ppermute(value, axis, pairs)


def per_device(
    acts,
    in_proj,
    out_proj,
    conv_weight,
    conv_bias,
    dt_bias,
    decay_rate,
    skip_gain,
    level_bias,
    norm_gain,
    gate_gain,
):
    n = lax.axis_size("seq")
    group = min(4, n)
    bits = group.bit_length() - 1
    position = lax.axis_index("seq")
    inner_at = lax.rem(position, group)
    hidden = acts[0].astype(f32)
    length = hidden.shape[0]
    inner = gate_gain.shape[1]
    heads = dt_bias.shape[1]
    head_size = inner // heads
    chans = conv_weight.shape[2]
    state = (chans - inner) // 2
    taps = conv_weight.shape[1]
    margin = taps - 1
    levels_all = level_bias.shape[1] // heads
    levels_used = n.bit_length() - 1
    wide = inner // group
    hs = heads // group
    tokens = group * length

    w = in_proj[0]
    rows = w.shape[0]

    def cut(lo, count):
        part = w[:, lo : lo + count].reshape(rows, group, count // group)
        return jnp.swapaxes(part, 0, 1)

    shared = jnp.broadcast_to(w[:, inner:chans][None], (group, rows, 2 * state))
    tail = hs + hs * levels_all
    used = 2 * wide + 2 * state + tail
    padded = -(-used // 128) * 128
    w_parts = jnp.concatenate(
        [
            cut(0, inner),
            shared,
            cut(chans, inner),
            cut(chans + inner, heads),
            cut(chans + inner + heads, heads * levels_all),
            jnp.zeros((group, rows, padded - used), w.dtype),
        ],
        axis=2,
    )
    u = (
        hidden * lax.rsqrt(jnp.mean(hidden * hidden, axis=1, keepdims=True) + EPS) * norm_gain[0]
    ).astype(bf16)
    u = jnp.swapaxes(u.reshape(length, n // group, group * rows), 0, 1)
    p = gathered(u, w_parts, n)

    def mine(vector, count):
        return lax.dynamic_slice_in_dim(vector, inner_at * count, count, axis=-1)

    mixed_ch = wide + 2 * state
    dims = (wide, state, head_size, taps)
    lasts = p[:, length - margin :, :mixed_ch]
    earlier = from_behind(lasts[group - 1 :], "seq", group)
    halo = jnp.concatenate([earlier, lasts[: group - 1]], axis=0).astype(f32)
    halo = jnp.pad(halo, ((0, 0), (-margin % 8, 0), (0, 0)))
    taps_w = jnp.concatenate([mine(conv_weight[0][:, :inner], wide), conv_weight[0][:, inner:]], 1)
    taps_b = jnp.concatenate([mine(conv_bias[0][:inner], wide), conv_bias[0][inner:]], 0)[None]
    lanes = padded - mixed_ch - wide
    small_bias = jnp.concatenate([mine(dt_bias[0], hs), mine(level_bias[0], hs * levels_all)])
    small_bias = jnp.pad(small_bias, (0, lanes - tail))[None]
    rate = jnp.pad(mine(decay_rate[0], hs), (0, lanes - hs))[None]
    skip = jnp.repeat(mine(skip_gain[0], hs), head_size)[None]

    def shaped(kind, *sizes):
        return jax.ShapeDtypeStruct((group,) + sizes, kind)

    x, bc, small, cum, states = per_block(
        functools.partial(state_kernel, dims),
        group,
        (p, halo),
        (taps_w, taps_b, small_bias, rate),
        (
            shaped(bf16, length, wide),
            shaped(bf16, length, 2 * state),
            shaped(f32, length, lanes),
            shaped(f32, length, lanes),
            shaped(f32, state, wide),
        ),
        2 * tokens * state * wide,
    )
    (y,) = per_block(
        functools.partial(inside_kernel, dims, levels_all),
        group,
        (x, bc, small, cum),
        (skip,),
        (shaped(f32, length, wide),),
        16 * tokens * length * wide,
    )
    ends = cum[:, length - 1, :hs]

    def faded(log, block):
        return jnp.exp(jnp.repeat(log, head_size))[None] * block

    buckets = [[] for _ in range(group)]
    summed = [states[b] for b in range(group)]
    logs = [ends[b] for b in range(group)]
    before = [jnp.zeros_like(ends[0]) for _ in range(group)]
    for bit in range(bits):
        half = 1 << bit
        merged, merged_logs = [], []
        for g in range(len(summed) // 2):
            low, high = summed[2 * g], summed[2 * g + 1]
            for b in range(2 * g * half, 2 * g * half + half):
                buckets[b].append(jnp.zeros_like(low))
            for b in range(2 * g * half + half, 2 * (g + 1) * half):
                buckets[b].append(faded(before[b], low))
                before[b] = before[b] + logs[2 * g]
            merged.append(faded(logs[2 * g + 1], low) + high)
            merged_logs.append(logs[2 * g] + logs[2 * g + 1])
        summed, logs = merged, merged_logs
    block_state, block_log = summed[0], logs[0]
    before_log = jnp.zeros_like(block_log)
    for bit in range(bits, levels_used):
        other_log, other_state = swapped((block_log, block_state.astype(bf16)), "seq", bit)
        other_state = other_state.astype(f32)
        upper = position >> bit & 1 == 1
        bucket = jnp.where(upper, faded(before_log, other_state), 0.0)
        for b in range(group):
            buckets[b].append(faded(before[b], bucket))
        merged_upper = faded(block_log, other_state) + block_state
        merged_lower = faded(other_log, block_state) + other_state
        block_state = jnp.where(upper, merged_upper, merged_lower)
        before_log = jnp.where(upper, before_log + other_log, before_log)
        block_log = block_log + other_log
    stacked = jnp.stack([jnp.stack(held) for held in buckets]).astype(bf16)
    (gated,) = per_block(
        functools.partial(outside_kernel, dims, levels_all, levels_used),
        group,
        (y, bc, stacked, small, cum, p),
        (),
        (shaped(bf16, length, wide),),
        2 * tokens * state * wide * levels_used,
    )

    own = exchanged(gated)
    own = jnp.swapaxes(own, 0, 1).reshape(length, inner).astype(f32)
    normed = (
        own * lax.rsqrt(jnp.mean(own * own, axis=1, keepdims=True) + EPS) * gate_gain[0]
    ).astype(bf16)
    result = (hidden + jnp.dot(normed, out_proj[0], preferred_element_type=f32)).astype(bf16)
    moved = passed_along(result, "section", 1)
    return moved[None]


def solution(mesh):
    return jax.shard_map(
        per_device,
        mesh=mesh,
        in_specs=(
            P("section", "seq", None),
            P("section", "seq", None),
            P("section", None, None),
            P("section", None, None),
            P("section", None),
            P("section", None),
            P("section", None),
            P("section", None),
            P("section", None),
            P("section", None),
            P("section", None),
        ),
        out_specs=P("section", "seq", None),
        check_vma=False,
    )
```

time: 226 us -> 204 us (0.903)
  Pallas kernels: 124 us -> 144 us
  matrix products: 22.3 us -> 5.73 us
  other arithmetic: 26.1 us -> 13.9 us
  waiting for transfers between devices: 13.6 us -> 2.66 us
  local copies, waits for them, and re-layouts: 32.1 us -> 28.4 us
    pallas_call x1 -> x4, Pallas kernels: 110 us -> 130 us  [the longest x1 114 us: gathered(): pl.pallas_call(functools.partial(gather_kernel, group, n), out_shape=jax....]
    dot_general x5 -> x0, matrix products: 16.5 us -> none  [the longest x1 9.7 us: per_device(): jnp.dot(u_all.reshape(tokens, -1), w_all.reshape(-1, padded), preferred_e...]
    ppermute x3, waiting for transfers between devices: 11 us -> 0.01 us  [swapped(): return lax.ppermute(block, axis, route)]
    another operation x11 -> x7, other arithmetic: 10.5 us -> 5.4 us  [the longest x6 4.69 us: per_device(): stacked = jnp.stack([jnp.stack(held) for held in buckets]).astype(bf16)]
    slice x15 -> x2, local copies, waits for them, and re-layouts: 5.77 us -> 1.49 us  [the longest x1 0.78 us: per_device(): halo = jnp.concatenate([earlier, lasts[:group - 1]], axis=0).astype(f32)]
    unnamed x83 -> x46, local copies, waits for them, and re-layouts: 6.24 us -> 9.26 us
    convert_element_type x4 -> x1, other arithmetic: 3.1 us -> 0.11 us  [per_device(): block_state.astype(bf16)]
    exp x1 -> x11, local copies, waits for them, and re-layouts: 0.77 us -> 3.7 us  [faded(): return jnp.exp(jnp.repeat(log, head_size))[None] * block]
  transfers between devices with their start and end apart: 5 -> 5, of which waited for: 3 -> 1; matrix products, arithmetic and copies ran while one was open for 11% -> 4% of each run, Pallas kernels for 0% -> 2%
where the time goes in v2:
time: 204 us; the launch traced here: 203 us
  Pallas kernels  144 us (71%)
  local copies, waits for them, and re-layouts  28.4 us (14%)
  other arithmetic  13.9 us (7%)
  starting transfers between devices  7.29 us (4%)
  matrix products  5.73 us (3%)
  waiting for transfers between devices  2.66 us (1%)
    pallas_call x1, Pallas kernels, gathered(): pl.pallas_call(functools.partial(gather_kernel, group, n), out_shape=jax....  114 us
    pallas_call x3, Pallas kernels, per_block(): pl.pallas_call(kernel, grid=(group,), out_shape=outs, in_specs=specs, out...  15.5 us
    pallas_call x1, Pallas kernels, exchanged(): pl.pallas_call(functools.partial(exchange_kernel, group), out_shape=jax.S...  14.4 us
    unnamed x46, local copies, waits for them, and re-layouts  9.26 us
    ppermute x3, starting transfers between devices, swapped(): return lax.ppermute(block, axis, route)  5.76 us
    dot_general x1, matrix products, per_device(): jnp.dot(normed, out_proj[0], preferred_element_type=f32)  5.73 us
    another operation x6, other arithmetic, per_device(): stacked = jnp.stack([jnp.stack(held) for held in buckets]).astype(bf16)  4.69 us
  transfers between devices with their start and end apart: 5, of which 1 were waited for; matrix products, arithmetic and copies ran while one was open for 4% of the time, Pallas kernels for 2%

profile of v2, /device:TPU:0, one launch (start us, length us, event | category | flops | bytes accessed | tf_op | source)
XLA Modules:
  0.0 202.8 jit_solution(16326406329117488534)
XLA Ops:
  0.0 2.3 %fusion.53 = (bf16[128,2048]{0,1:T(8,128)(2,1)}, bf16[128,2048]{0,1:T(8,128)(2,1)}) fusion(bf16[128,4640]{0,1:T(8,128)(2,1)} %bitcast.125), kind=kLoop, calls=%fused_computation.97 | loop fusion | bytes 2097152 | tf_op jit(solution)/shard_map/slice | solution.py:466
  4.8 1.2 copy.15
  6.0 1.2 copy.17
  9.0 1.9 copy.14
  10.9 2.8 %fusion.12.u_ref = bf16[4,256,512]{2,1,0:T(8,128)(2,1)} fusion(f32[256,4,512]{2,0,1:T(8,128)} %copy.14, f32[4,512]{1,0:T(4,128)S(1)} %mul.170, f32[256]{0:T(256)S(1)} %add_rsqrt_fusion.1), kind=kLoop, calls=%fused_computation.13 | loop fusion | flops 1572864 | bytes 3154944 | tf_op jit(solution)/shard_map/transpose | solution.py:487
  13.8 1.9 concatenate.15.w_ref
  15.7 114.4 %shard_map.109.p_ref = bf16[4,256,1408]{2,1,0:T(8,128)(2,1)} custom-call(bf16[4,256,512]{2,1,0:T(8,128)(2,1)} %fusion.12.u_ref, bf16[4,128,1408]{2,1,0:T(8,128)(2,1)} %concatenate.15.w_ref), custom_call_target="tpu_custom_call" | custom-call | tf_op jit(solution)/shard_map/pallas_call | solution.py:212
  130.8 1.5 collective-permute-start
  135.0 1.8 copy-done.1
  136.8 6.3 %shard_map.110 = (bf16[4,256,512]{2,1,0:T(8,128)(2,1)S(1)}, bf16[4,256,256]{2,1,0:T(8,128)(2,1)S(1)}, f32[4,256,128]{2,1,0:T(8,128)S(1)}, f32[4,256,128]{2,1,0:T(8,128)S(1)}, f32[4,128,512]{2,1,0:T(8,128)S(1)}) custom-call(bf16[4,256,1408]{2,1,0:T(8,128)(2,1)S(1)} %copy-done.1, f32[4,8,768]{2,1,0:T(8,128)S(1)} %fusion.39.halo_ref, ...), custom_call_target="tpu_custom_call" | custom-call | flops 134217728 | bytes 2998272 | tf_op jit(solution)/shard_map/pallas_call | solution.py:358
  146.2 1.2 collective-permute-start.2
  151.9 1.6 fusion.34
  153.5 3.7 %collective-permute-start.3 = (bf16[128,512]{1,0:T(8,128)(2,1)}, bf16[128,512]{1,0:T(8,128)(2,1)}, u32[]{:S(2)}, u32[]{:S(2)}) collective-permute-start(bf16[128,512]{1,0:T(8,128)(2,1)} %get-tuple-element.41), channel_id=1, source_target_pairs={{0,8},{8,0},{1,9},{9,1},{2,10},{10,2},{3,11},{11,3},{4,12},{12,4},... | collective-permute-start | bytes 393224 | tf_op jit(solution)/shard_map/ppermute | solution.py:414
  157.2 1.0 copy-done.5
  158.2 1.2 copy-done.8
  159.5 4.2 %shard_map.111.y_ref = f32[4,256,512]{2,1,0:T(8,128)S(1)} custom-call(bf16[4,256,512]{2,1,0:T(8,128)(2,1)S(1)} %copy-done.8, bf16[4,256,256]{2,1,0:T(8,128)(2,1)S(1)} %get-tuple-element.11.bc_ref, f32[4,256,128]{2,1,0:T(8,128)S(1)} %copy-done.5, f32[4,256,128]{2,1,0:T(8,128)S(1)} %get-tuple-element.13.cum_ref, f32[1,512]{1,0:T(1,128)S(1)} %broadcast_in_dim_reshape.3.skip_ref), custom_call_target="tpu_custom_call" | custom-call | flops 2147483648 | bytes 2623488 | tf_op jit(solution)/shard_map/pallas_call | solution.py:358
  164.4 1.1 fusion.27
  167.6 1.5 copy-done.2
  169.3 5.0 %shard_map.112.x_ref = bf16[4,256,512]{2,1,0:T(8,128)(2,1)S(1)} custom-call(f32[4,256,512]{2,1,0:T(8,128)S(1)} %shard_map.111.y_ref, bf16[4,256,256]{2,1,0:T(8,128)(2,1)S(1)} %get-tuple-element.11.bc_ref, bf16[4,4,128,512]{3,2,1,0:T(8,128)(2,1)S(1)} %pad_maximum_fusion.bucket_ref, f32[4,256,128]{2,1,0:T(8,128)S(1)} %copy-done.6, ...), custom_call_target="tpu_custom_call" | custom-call | flops 536870912 | bytes 8650752 | tf_op jit(solution)/shard_map/pallas_call | solution.py:358
  175.2 14.4 %shard_map.113 = bf16[4,256,512]{2,1,0:T(8,128)(2,1)} custom-call(bf16[4,256,512]{2,1,0:T(8,128)(2,1)} %copy-done.3), custom_call_target="tpu_custom_call" | custom-call | tf_op jit(solution)/shard_map/pallas_call | solution.py:397
  189.7 1.5 fusion.8
  191.2 1.6 fusion.13
  193.4 5.7 %fusion.5 = bf16[256,2048]{1,0:T(8,128)(2,1)S(1)} fusion(bf16[256,2048]{0,1:T(8,128)(2,1)S(1)} %bitcast.120, bf16[1,2048,2048]{2,1,0:T(8,128)(2,1)} %param.13, bf16[1,256,2048]{2,1,0:T(8,128)(2,1)S(1)} %copy-done.10), kind=kOutput, calls=%fused_computation.5 | convolution fusion | flops 2149056512 | bytes 11534336 | tf_op jit(solution)/shard_map/dot_general | solution.py:583
  199.2 2.6 %collective-permute-done.4 = bf16[256,2048]{1,0:T(8,128)(2,1)S(1)} collective-permute-done((bf16[256,2048]{1,0:T(8,128)(2,1)S(1)}, bf16[256,2048]{1,0:T(8,128)(2,1)S(1)}, u32[]{:S(2)}, u32[]{:S(2)}) %collective-permute-start.4) | collective-permute-done | bytes 1048608 | tf_op jit(solution)/shard_map/ppermute | solution.py:426
  (118 shorter events, 20.5 us)
Async XLA Ops:
  0.0 132.6 %copy-start = (f32[1,256]{1,0:T(1,128)S(1)}, f32[1,256]{1,0:T(1,128)}, u32[]{:S(2)}) copy-start(f32[1,256]{1,0:T(1,128)} %param.19) | copy-start | bytes 3076
  0.0 3.9 %copy-start.9 = (bf16[1,256,2048]{2,1,0:T(8,128)(2,1)S(1)}, bf16[1,256,2048]{2,1,0:T(8,128)(2,1)}, u32[]{:S(2)}) copy-start(bf16[1,256,2048]{2,1,0:T(8,128)(2,1)} %param.11) | copy-start | bytes 3145732
  4.5 3.8 %copy-start.16 = (f32[1,2048]{1,0:T(1,128)S(1)}, f32[1,2048]{1,0:T(1,128)}, u32[]{:S(2)}) copy-start(f32[1,2048]{1,0:T(1,128)} %param.20) | copy-start | bytes 24580
  15.7 116.6 %copy-start.15 = (f32[1,4,2304]{2,1,0:T(4,128)S(1)}, f32[1,4,2304]{2,1,0:T(4,128)}, u32[]{:S(2)}) copy-start(f32[1,4,2304]{2,1,0:T(4,128)} %param.14) | copy-start | bytes 110596
  15.7 116.7 %copy-start.19 = (f32[1,32]{1,0:T(1,128)S(1)}, f32[1,32]{1,0:T(1,128)}, u32[]{:S(2)}) copy-start(f32[1,32]{1,0:T(1,128)} %param.16) | copy-start | bytes 388
  15.7 116.7 %copy-start.20 = (f32[1,32]{1,0:T(1,128)S(1)}, f32[1,32]{1,0:T(1,128)}, u32[]{:S(2)}) copy-start(f32[1,32]{1,0:T(1,128)} %param.17) | copy-start | bytes 388
  15.7 116.8 %slice-start = ((f32[1,2304]{1,0:T(1,128)}), f32[1,2048]{1,0:T(1,128)S(1)}, s32[]{:S(2)}) async-start(f32[1,2304]{1,0:T(1,128)} %param.15), calls=%async_computation | async-start | bytes 16384 | tf_op jit(solution)/shard_map/slice | solution.py:500
  15.7 116.8 %copy-start.21 = (f32[1,32]{1,0:T(1,128)S(1)}, f32[1,32]{1,0:T(1,128)}, u32[]{:S(2)}) copy-start(f32[1,32]{1,0:T(1,128)} %param.18) | copy-start | bytes 388
  15.7 116.9 %slice-start.1 = ((f32[1,2304]{1,0:T(1,128)}), f32[1,256]{1,0:T(1,128)S(1)}, s32[]{:S(2)}) async-start(f32[1,2304]{1,0:T(1,128)} %param.15), calls=%async_computation.1 | async-start | bytes 2048 | tf_op jit(solution)/shard_map/slice | solution.py:500
  15.7 118.0 %copy-start.17 = (f32[1,2048]{1,0:T(1,128)S(1)}, f32[1,2048]{1,0:T(1,128)}, u32[]{:S(2)}) copy-start(f32[1,2048]{1,0:T(1,128)} %param.21) | copy-start | bytes 24580
  130.8 4.1 %collective-permute-start = (bf16[1,3,768]{2,1,0:T(4,128)(2,1)S(1)}, bf16[1,3,768]{2,1,0:T(4,128)(2,1)S(1)}, u32[]{:S(2)}, u32[]{:S(2)}) collective-permute-start(bf16[1,3,768]{2,1,0:T(4,128)(2,1)S(1)} %slice.78), channel_id=1, source_target_pairs={{0,4},{1,5},{2,6},{3,7},{4,8},{5,9},{6,10},{7,11},{8,12},{9,13},{1... | collective-permute-start | bytes 13832 | tf_op jit(solution)/shard_map/ppermute | solution.py:420
  134.9 1.8 copy-start.1
  144.0 13.2 %copy-start.4 = (f32[4,256,128]{2,1,0:T(8,128)}, f32[4,256,128]{2,1,0:T(8,128)S(1)}, u32[]{:S(2)}) copy-start(f32[4,256,128]{2,1,0:T(8,128)S(1)} %get-tuple-element.12.small_ref) | copy-start | bytes 1572868
  145.3 6.6 %collective-permute-start.1 = (bf16[128,512]{1,0:T(8,128)(2,1)S(1)}, bf16[128,512]{1,0:T(8,128)(2,1)S(1)}, u32[]{:S(2)}, u32[]{:S(2)}) collective-permute-start(bf16[128,512]{1,0:T(8,128)(2,1)S(1)} %get-tuple-element.17), channel_id=1, source_target_pairs={{0,4},{4,0},{1,5},{5,1},{2,6},{6,2},{3,7},{7,3},{8,12},{12,8},{9,1... | collective-permute-start | bytes 393224 | tf_op jit(solution)/shard_map/ppermute | solution.py:414
  146.2 5.0 %collective-permute-start.2 = (f32[8]{0:T(128)S(1)}, f32[8]{0:T(128)S(1)}, u32[]{:S(2)}, u32[]{:S(2)}) collective-permute-start(f32[8]{0:T(128)S(1)} %get-tuple-element.16), channel_id=1, source_target_pairs={{0,4},{4,0},{1,5},{5,1},{2,6},{6,2},{3,7},{7,3},{8,12},{12,8},{9,1... | collective-permute-start | bytes 104 | tf_op jit(solution)/shard_map/ppermute | solution.py:414
  153.5 10.9 %collective-permute-start.3 = (bf16[128,512]{1,0:T(8,128)(2,1)}, bf16[128,512]{1,0:T(8,128)(2,1)}, u32[]{:S(2)}, u32[]{:S(2)}) collective-permute-start(bf16[128,512]{1,0:T(8,128)(2,1)} %get-tuple-element.41), channel_id=1, source_target_pairs={{0,8},{8,0},{1,9},{9,1},{2,10},{10,2},{3,11},{11,3},{4,12},{12,4},... | collective-permute-start | bytes 393224 | tf_op jit(solution)/shard_map/ppermute | solution.py:414
  159.5 4.2 %copy-start.18 = (f32[8]{0:T(128)S(1)}, f32[8]{0:T(128)}, u32[]{:S(2)}) copy-start(f32[8]{0:T(128)} %get-tuple-element.45) | copy-start | bytes 100
  164.4 2.8 %copy-start.11 = (bf16[1,128,512]{2,1,0:T(8,128)(2,1)S(1)}, bf16[1,128,512]{2,1,0:T(8,128)(2,1)}, u32[]{:S(2)}) copy-start(bf16[1,128,512]{2,1,0:T(8,128)(2,1)} %get-tuple-element.25) | copy-start | bytes 393220
  164.4 2.8 %copy-start.12 = (bf16[1,128,512]{2,1,0:T(8,128)(2,1)S(1)}, bf16[1,128,512]{2,1,0:T(8,128)(2,1)}, u32[]{:S(2)}) copy-start(bf16[1,128,512]{2,1,0:T(8,128)(2,1)} %get-tuple-element.23) | copy-start | bytes 393220
  164.4 2.8 %copy-start.13 = (bf16[1,128,512]{2,1,0:T(8,128)(2,1)S(1)}, bf16[1,128,512]{2,1,0:T(8,128)(2,1)}, u32[]{:S(2)}) copy-start(bf16[1,128,512]{2,1,0:T(8,128)(2,1)} %get-tuple-element.39) | copy-start | bytes 393220
  164.4 2.8 %copy-start.14 = (bf16[1,128,512]{2,1,0:T(8,128)(2,1)S(1)}, bf16[1,128,512]{2,1,0:T(8,128)(2,1)}, u32[]{:S(2)}) copy-start(bf16[1,128,512]{2,1,0:T(8,128)(2,1)} %get-tuple-element.42) | copy-start | bytes 393220
  167.4 1.9 copy-start.6
  191.2 2.2 %copy-start.10 = (bf16[1,256,2048]{2,1,0:T(8,128)(2,1)S(1)}, bf16[1,256,2048]{2,1,0:T(8,128)(2,1)}, u32[]{:S(2)}) copy-start(bf16[1,256,2048]{2,1,0:T(8,128)(2,1)} %param.11) | copy-start | bytes 3145732
  199.1 2.7 %collective-permute-start.4 = (bf16[256,2048]{1,0:T(8,128)(2,1)S(1)}, bf16[256,2048]{1,0:T(8,128)(2,1)S(1)}, u32[]{:S(2)}, u32[]{:S(2)}) collective-permute-start(bf16[256,2048]{1,0:T(8,128)(2,1)S(1)} %fusion.5), channel_id=1, source_target_pairs={{0,16},{16,0},{1,17},{17,1},{2,18},{18,2},{3,19},{19,3},{4,20},{20... | collective-permute-start | bytes 3145736 | tf_op jit(solution)/shard_map/ppermute | solution.py:426
  (5 other events, 6.0 us)

commit v3 on v2

--- a/solution.py
+++ b/solution.py
@@ -31,15 +31,22 @@
 
 
 def gather_kernel(
-    group, n, u_ref, w_ref, p_ref, u_all, w_all, acc, u_send, u_recv, w_send, up_send, down_send, w_recv, own_sem
+    group, n, starts, u_ref, w_ref, tail_ref, p_ref, halo_ref,
+    u_all, w_all, acc, u_send, u_recv, w_send, up_send, down_send, w_recv,
+    bc_up, bc_down, bc_peer, bc_recv, own_sem, halo_sem
 ):
     me = lax.axis_index("seq")
     outer = me // group
     inner = lax.rem(me, group)
     outers = n // group
     base = outer * group
-    length = u_ref.shape[1]
-    rows = w_ref.shape[1]
+    length = u_ref.shape[0]
+    rows = w_ref.shape[0]
+    depth = group * rows
+    wide, bc_from, z_from = starts
+    lanes = tail_ref.shape[2]
+    main = 2 * wide + lanes
+    columns = w_all.shape[2]
     has_up = outer < outers - 1
     has_down = outer > 0
     barrier = pltpu.get_barrier_semaphore()
@@ -58,78 +65,134 @@
         barrier, group - 1 + has_up.astype(jnp.int32) + has_down.astype(jnp.int32)
     )
 
-    def w_slot(source, slot):
-        return w_all.at[source, pl.ds(pl.multiple_of(slot * rows, rows), rows), :]
-
-    def u_slot(slot):
-        return u_all.at[:, slot]
-
-    own_w = pltpu.make_async_copy(w_ref.at[inner], w_slot(outer, inner), own_sem.at[0])
-    own_w.start()
-    own_u = pltpu.make_async_copy(u_ref, u_slot(inner), own_sem.at[1])
+    def slot_at(source, slot, lo, hi):
+        return w_all.at[source, pl.ds(pl.multiple_of(slot * rows, rows), rows), lo:hi]
+
+    def main_slot(source, slot):
+        return slot_at(source, slot, 0, main)
+
+    def bc_slot(source, slot):
+        return slot_at(source, slot, main, columns)
+
+    def parts_for(peer):
+        at = pl.multiple_of(peer * wide, wide)
+        return (
+            (w_ref.at[:, pl.ds(at, wide)], 0, wide),
+            (w_ref.at[:, pl.ds(pl.multiple_of(z_from + at, 128), wide)], wide, 2 * wide),
+            (tail_ref.at[peer], 2 * wide, main),
+        )
+
+    bc_src = w_ref.at[:, bc_from : bc_from + columns - main]
+
+    def up(source, slot):
+        at = source * group + slot
+        piece = main_slot(source, slot)
+        return remote(piece, piece, up_send.at[at], w_recv.at[at], me + group)
+
+    def down(source, slot):
+        at = source * group + slot
+        piece = main_slot(source, slot)
+        return remote(piece, piece, down_send.at[at], w_recv.at[at], me - group)
+
+    def along(source, step):
+        piece = bc_slot(source, inner)
+        here = bc_recv.at[source * group + inner]
+        if step > 0:
+            return remote(piece, piece, bc_up.at[source], here, me + group)
+        return remote(piece, piece, bc_down.at[source], here, me - group)
+
+    def across(source, step):
+        piece = bc_slot(source, inner)
+        peer = base + lax.rem(inner + step, group)
+        at = source * group
+        return remote(piece, piece, bc_peer.at[at + step], bc_recv.at[at + inner], peer)
+
+    def arrived(source, slot):
+        piece = main_slot(source, slot)
+        remote(piece, piece, w_send.at[0], w_recv.at[source * group + slot], me).wait_recv()
+
+    def bc_arrived(source, slot):
+        piece = bc_slot(source, slot)
+        remote(piece, piece, w_send.at[0], bc_recv.at[source * group + slot], me).wait_recv()
+
+    for src, lo, hi in parts_for(inner):
+        pltpu.make_async_copy(src, slot_at(outer, inner, lo, hi), own_sem.at[0]).start()
+    pltpu.make_async_copy(bc_src, bc_slot(outer, inner), own_sem.at[0]).start()
+    own_u = pltpu.make_async_copy(u_ref, u_all.at[inner], own_sem.at[1])
     own_u.start()
-
-    def up(src, source, slot):
-        at = source * group + slot
-        return remote(src, w_slot(source, slot), up_send.at[at], w_recv.at[at], me + group)
-
-    def down(src, source, slot):
-        at = source * group + slot
-        return remote(src, w_slot(source, slot), down_send.at[at], w_recv.at[at], me - group)
-
-    def arrived(source, slot):
-        piece = w_slot(source, slot)
-        remote(piece, piece, w_send.at[0], w_recv.at[source * group + slot], me).wait_recv()
+    for step in range(1, group):
+        peer = lax.rem(inner + step, group)
+        for src, lo, hi in parts_for(peer):
+            remote(
+                src, slot_at(outer, inner, lo, hi), w_send.at[step], w_recv.at[me], base + peer
+            ).start()
+    whole_slot = slot_at(outer, inner, 0, columns)
+    pltpu.make_async_copy(whole_slot, whole_slot, own_sem.at[0]).wait()
+
+    @pl.when(has_up)
+    def _():
+        up(outer, inner).start()
+        along(outer, 1).start()
+
+    @pl.when(has_down)
+    def _():
+        down(outer, inner).start()
+        along(outer, -1).start()
+
+    for step in range(1, group):
+        slot = lax.rem(inner + step, group)
+        arrived(outer, slot)
+
+        @pl.when(has_up)
+        def _():
+            up(outer, slot).start()
+
+        @pl.when(has_down)
+        def _():
+            down(outer, slot).start()
 
     sends = []
     for step in range(1, group):
         peer = lax.rem(inner + step, group)
-        copy = remote(
-            w_ref.at[peer], w_slot(outer, inner), w_send.at[step], w_recv.at[me], base + peer
-        )
+        copy = remote(u_ref, u_all.at[inner], u_send.at[step], u_recv.at[inner], base + peer)
         copy.start()
         sends.append(copy)
-
-    @pl.when(has_up)
-    def _():
-        up(w_ref.at[inner], outer, inner).start()
-
-    @pl.when(has_down)
-    def _():
-        down(w_ref.at[inner], outer, inner).start()
-
-    for step in range(1, group):
-        slot = lax.rem(inner + step, group)
-        arrived(outer, slot)
-
-        @pl.when(has_up)
-        def _():
-            up(w_slot(outer, slot), outer, slot).start()
-
-        @pl.when(has_down)
-        def _():
-            down(w_slot(outer, slot), outer, slot).start()
-
-    for step in range(1, group):
-        peer = lax.rem(inner + step, group)
-        copy = remote(u_ref, u_slot(inner), u_send.at[step], u_recv.at[inner], base + peer)
-        copy.start()
-        sends.append(copy)
+        across(outer, step).start()
+
+    chunked = depth % 128 == 0
 
     def multiply(source, block, first=False):
-        part = jnp.dot(u_all[source, block], w_all[source], preferred_element_type=f32)
+        if not chunked:
+            return
+
+        at = pl.multiple_of(source * depth, 128)
+        part = jnp.dot(
+            u_all[block, :, pl.ds(at, depth)], w_all[source], preferred_element_type=f32
+        )
         if first:
             acc[block] = part
         else:
             acc[block] += part
 
+    def ready(source):
+        for step in range(1, group):
+            bc_arrived(source, lax.rem(inner + step, group))
+
     def multiply_both(distance, block):
         @pl.when(outer - distance >= 0)
         def _():
+            @pl.when(block == 0)
+            def _():
+                ready(outer - distance)
+
             multiply(outer - distance, block)
 
         @pl.when(outer + distance < outers)
         def _():
+            @pl.when(block == 0)
+            def _():
+                ready(outer + distance)
+
             multiply(outer + distance, block)
 
     def relay(distance, block):
@@ -137,19 +200,43 @@
 
         @pl.when(outer - distance >= 0)
         def _():
-            arrived(outer - distance, slot)
+            source = outer - distance
+            arrived(source, slot)
 
             @pl.when(has_up)
             def _():
-                up(w_slot(outer - distance, slot), outer - distance, slot).start()
+                up(source, slot).start()
+
+            @pl.when(block == 0)
+            def _():
+                bc_arrived(source, inner)
+
+                @pl.when(has_up)
+                def _():
+                    along(source, 1).start()
+
+                for step in range(1, group):
+                    across(source, step).start()
 
         @pl.when(outer + distance < outers)
         def _():
-            arrived(outer + distance, slot)
+            source = outer + distance
+            arrived(source, slot)
 
             @pl.when(has_down)
             def _():
-                down(w_slot(outer + distance, slot), outer + distance, slot).start()
+                down(source, slot).start()
+
+            @pl.when(block == 0)
+            def _():
+                bc_arrived(source, inner)
+
+                @pl.when(has_down)
+                def _():
+                    along(source, -1).start()
+
+                for step in range(1, group):
+                    across(source, step).start()
 
     def relay_first(block, carry):
         relay(1, block)
@@ -157,11 +244,11 @@
 
     if outers > 1:
         lax.fori_loop(0, group, relay_first, 0)
-    own_w.wait()
     own_u.wait()
     for step in range(1, group):
         peer = lax.rem(inner + step, group)
-        remote(u_slot(peer), u_slot(peer), u_send.at[0], u_recv.at[peer], me).wait_recv()
+        remote(u_all.at[peer], u_all.at[peer], u_send.at[0], u_recv.at[peer], me).wait_recv()
+    ready(outer)
 
     def own_work(block, carry):
         multiply(outer, block, True)
@@ -178,13 +265,28 @@
 
     lax.fori_loop(2 * group, outers * group, later, 0)
 
-    def finish(block, carry):
+    def finish(step, carry):
         if outers > 1:
-            multiply_both(outers - 1, block)
-        p_ref[block] = acc[block].astype(p_ref.dtype)
+            multiply_both(outers - 1, step)
+        if chunked:
+            p_ref[step] = acc[step].astype(p_ref.dtype)
         return carry
 
     lax.fori_loop(0, group, finish, 0)
+    if not chunked:
+        every = w_all[...].reshape(outers * depth, columns)
+
+        def at_once(block, carry):
+            part = jnp.dot(u_all[block], every, preferred_element_type=f32)
+            p_ref[block] = part.astype(p_ref.dtype)
+            return carry
+
+        lax.fori_loop(0, group, at_once, 0)
+    keep = halo_ref.shape[0]
+
+    @pl.when(jnp.logical_not(has_down))
+    def _():
+        halo_ref[...] = jnp.zeros(halo_ref.shape, halo_ref.dtype)
 
     def drain(at, carry):
         source = at // group
@@ -192,30 +294,68 @@
 
         @pl.when(jnp.logical_and(has_up, source <= outer))
         def _():
-            up(w_slot(source, slot), source, slot).wait_send()
+            up(source, slot).wait_send()
+
+            @pl.when(slot == 0)
+            def _():
+                along(source, 1).wait_send()
 
         @pl.when(jnp.logical_and(has_down, source >= outer))
         def _():
-            down(w_slot(source, slot), source, slot).wait_send()
+            down(source, slot).wait_send()
+
+            @pl.when(slot == 0)
+            def _():
+                along(source, -1).wait_send()
+
+        @pl.when(slot == 0)
+        def _():
+            for step in range(1, group):
+                across(source, step).wait_send()
 
         return carry
 
     lax.fori_loop(0, n, drain, 0)
+    edge = remote(
+        p_ref.at[group - 1, length - keep :], halo_ref, halo_sem.at[0], halo_sem.at[1], me + group
+    )
+
+    @pl.when(has_up)
+    def _():
+        edge.start()
+
     for copy in sends:
         copy.wait_send()
-
-
-def gathered(u, w_parts, n):
-    group, rows, columns = w_parts.shape
-    outers, length, depth = u.shape
+    for step in range(1, group):
+        piece = main_slot(outer, inner)
+        remote(piece, piece, w_send.at[step], w_recv.at[me], me).wait_send()
+
+    @pl.when(has_up)
+    def _():
+        edge.wait_send()
+
+    @pl.when(has_down)
+    def _():
+        edge.wait_recv()
+
+
+def gathered(u, w, tails, n, starts):
+    group, rows, lanes = tails.shape
+    length = u.shape[0]
+    outers = n // group
+    wide, bc_from, z_from = starts
+    columns = 2 * wide + lanes + z_from - bc_from
     dma = pltpu.SemaphoreType.DMA
     return pl.pallas_call(
-        functools.partial(gather_kernel, group, n),
-        out_shape=jax.ShapeDtypeStruct((group, length, columns), bf16),
-        in_specs=[pl.BlockSpec(memory_space=pltpu.VMEM)] * 2,
-        out_specs=pl.BlockSpec(memory_space=pltpu.VMEM),
+        functools.partial(gather_kernel, group, n, starts),
+        out_shape=(
+            jax.ShapeDtypeStruct((group, length, columns), bf16),
+            jax.ShapeDtypeStruct((16, columns), bf16),
+        ),
+        in_specs=[pl.BlockSpec(memory_space=pltpu.VMEM)] * 3,
+        out_specs=[pl.BlockSpec(memory_space=pltpu.VMEM)] * 2,
         scratch_shapes=[
-            pltpu.VMEM((outers, group, length, depth), bf16),
+            pltpu.VMEM((group,) + u.shape, bf16),
             pltpu.VMEM((outers, group * rows, columns), bf16),
             pltpu.VMEM((group, length, columns), f32),
             dma((group,)),
@@ -224,12 +364,17 @@
             dma((n,)),
             dma((n,)),
             dma((n,)),
+            dma((outers,)),
+            dma((outers,)),
+            dma((n,)),
+            dma((n,)),
+            dma((2,)),
             dma((2,)),
         ],
         compiler_params=pltpu.CompilerParams(
             collective_id=0, has_side_effects=True, vmem_limit_bytes=56 << 20
         ),
-    )(u, w_parts)
+    )(u, w, tails)
 
 
 def selector(lanes, wide, size, first, stride):
@@ -255,14 +400,19 @@
 
 
 def state_kernel(
-    dims, p_ref, halo_ref, taps_ref, bias_ref, small_bias_ref, rate_ref, x_ref, bc_ref, small_ref, cum_ref, state_ref
+    dims, p_ref, before_ref, halo_ref, taps_ref, bias_ref, small_bias_ref, rate_ref, x_ref, bc_ref, small_ref, cum_ref, state_ref
 ):
     wide, state, size, taps = dims
-    mixed_ch = wide + 2 * state
     length = p_ref.shape[1]
-    raw = p_ref[0, :, :mixed_ch].astype(f32)
-    ext = jnp.concatenate([halo_ref[0], raw], axis=0)
-    first = halo_ref.shape[1] - taps + 1
+    main = p_ref.shape[2] - 2 * state
+    keep = halo_ref.shape[0]
+    raw = jnp.concatenate([p_ref[0, :, :wide], p_ref[0, :, main:]], axis=1).astype(f32)
+    last = jnp.where(
+        pl.program_id(0) == 0, halo_ref[...].astype(f32), before_ref[0].astype(f32)
+    )
+    last = jnp.concatenate([last[:, :wide], last[:, main:]], axis=1)
+    ext = jnp.concatenate([last, raw], axis=0)
+    first = keep - taps + 1
     mixed = bias_ref[...] + taps_ref[taps - 1 :] * raw
     for k in range(taps - 1):
         mixed = mixed + taps_ref[k : k + 1] * ext[first + k : first + k + length]
@@ -271,7 +421,7 @@
     x_ref[0] = x.astype(bf16)
     bc = mixed[:, wide:].astype(bf16)
     bc_ref[0] = bc
-    small = softplus(p_ref[0, :, mixed_ch + wide :].astype(f32) + small_bias_ref[...])
+    small = softplus(p_ref[0, :, 2 * wide : main].astype(f32) + small_bias_ref[...])
     small_ref[0] = small
     rows = lax.broadcasted_iota(jnp.int32, (length, length), 0)
     cols = lax.broadcasted_iota(jnp.int32, (length, length), 1)
@@ -323,22 +473,98 @@
     y_ref[0] = y * own + skip_ref[...] * x
 
 
-def outside_kernel(dims, levels, used, y_ref, bc_ref, bucket_ref, small_ref, cum_ref, p_ref, q_ref):
+def outside_kernel(
+    dims, levels, used, group, y_ref, bc_ref, bucket_ref, small_ref, cum_ref, p_ref, acts_ref, gain_ref, w_hbm,
+    out_ref, q_own, q_got, w_ref, acc, w_sem, send_sem, recv_sem
+):
     wide, state, size, _ = dims
     hs = wide // size
     lanes = small_ref.shape[2]
-    c = bc_ref[0, :, state:]
-    small = small_ref[0]
-    total = None
-    for level in range(used):
-        reads = jnp.dot(c, bucket_ref[0, level], preferred_element_type=f32)
-        term = reads * spread(small, selector(lanes, wide, size, hs + level + 1, levels))
-        total = term if total is None else total + term
-    y = y_ref[0]
-    if total is not None:
-        y = y + total * spread(jnp.exp(cum_ref[0]), selector(lanes, wide, size, 0, 1))
-    at = wide + 2 * state
-    q_ref[0] = (y * silu(p_ref[0, :, at : at + wide].astype(f32))).astype(bf16)
+    me = lax.axis_index("seq")
+    inner = lax.rem(me, group)
+    base = me - inner
+    load = pltpu.make_async_copy(w_hbm, w_ref, w_sem)
+    load.start()
+    for step in range(1, group):
+        greet(base + lax.rem(inner + step, group))
+    pl.semaphore_wait(pltpu.get_barrier_semaphore(), group - 1)
+
+    def copy_to(step):
+        peer = lax.rem(inner + step, group)
+        return remote(
+            q_own.at[peer], q_got.at[inner], send_sem.at[step], recv_sem.at[inner], base + peer
+        )
+
+    def work(step, carry):
+        block = lax.rem(inner + step, group)
+        c = bc_ref[block, :, state:]
+        small = small_ref[block]
+        total = None
+        for level in range(used):
+            reads = jnp.dot(c, bucket_ref[block, level], preferred_element_type=f32)
+            term = reads * spread(small, selector(lanes, wide, size, hs + level + 1, levels))
+            total = term if total is None else total + term
+        y = y_ref[block]
+        if total is not None:
+            y = y + total * spread(jnp.exp(cum_ref[block]), selector(lanes, wide, size, 0, 1))
+        z = p_ref[block, :, wide : 2 * wide].astype(f32)
+        q_own[block] = (y * silu(z)).astype(bf16)
+
+        @pl.when(step > 1)
+        def _():
+            copy_to(step - 1).start()
+
+        return carry
+
+    lax.fori_loop(1, group + 1, work, 0)
+    load.wait()
+
+    def project(q, j):
+        q = q.astype(f32)
+        part = jnp.dot(
+            (q * gain_ref[j]).astype(bf16), w_ref[j], preferred_element_type=f32
+        )
+        return part, jnp.sum(q * q, axis=1, keepdims=True)
+
+    acc[...], squares = project(q_own[inner], inner)
+
+    def add(step, squares):
+        peer = lax.rem(inner + step, group)
+        remote(q_got.at[peer], q_got.at[peer], send_sem.at[0], recv_sem.at[peer], me).wait_recv()
+        part, more = project(q_got[peer], peer)
+        acc[...] += part
+        return squares + more
+
+    squares = lax.fori_loop(1, group, add, squares)
+    scale = lax.rsqrt(squares / (wide * group) + EPS)
+    out_ref[...] = (acts_ref[...].astype(f32) + acc[...] * scale).astype(bf16)
+    for step in range(1, group):
+        copy_to(step).wait_send()
+
+
+def finished(dims, levels, used, args, acts, gains, w):
+    group, wide, width = w.shape
+    length = acts.shape[0]
+    dma = pltpu.SemaphoreType.DMA
+    vmem = pl.BlockSpec(memory_space=pltpu.VMEM)
+    return pl.pallas_call(
+        functools.partial(outside_kernel, dims, levels, used, group),
+        out_shape=jax.ShapeDtypeStruct((length, width), bf16),
+        in_specs=[vmem] * 8 + [pl.BlockSpec(memory_space=pl.ANY)],
+        out_specs=vmem,
+        scratch_shapes=[
+            pltpu.VMEM((group, length, wide), bf16),
+            pltpu.VMEM((group, length, wide), bf16),
+            pltpu.VMEM(w.shape, bf16),
+            pltpu.VMEM((length, width), f32),
+            dma,
+            dma((group,)),
+            dma((group,)),
+        ],
+        compiler_params=pltpu.CompilerParams(
+            collective_id=1, has_side_effects=True, vmem_limit_bytes=48 << 20
+        ),
+    )(*args, acts, gains, w)
 
 
 def blocked(shape):
@@ -351,9 +577,17 @@
     return pl.BlockSpec(tuple(shape), lambda b: (0,) * rest)
 
 
-def per_block(kernel, group, split, fixed, outs, flops):
+def per_block(kernel, group, split, fixed, outs, flops, edge=0):
+    specs = [blocked(v.shape) for v in split]
+    if edge:
+        p = split[0]
+        at = p.shape[1] // edge - 1
+        specs.append(
+            pl.BlockSpec((1, edge, p.shape[2]), lambda b: (jnp.maximum(b - 1, 0), at, 0))
+        )
+        split = split + (p,)
     order = split + fixed
-    specs = [blocked(v.shape) for v in split] + [whole(v.shape) for v in fixed]
+    specs += [whole(v.shape) for v in fixed]
     moved = sum(v.size * v.dtype.itemsize for v in order)
     return pl.pallas_call(
         kernel,
@@ -411,12 +645,6 @@
         high = low | 1 << apart
         if high != low and high < count:
             route += [(low, high), (high, low)]
-    return lax.ppermute(block, axis, route)
-
-
-def from_behind(block, axis, distance):
-    devices = range(lax.axis_size(axis))
-    route = [(i - distance, i) for i in devices if i - distance in devices]
     return lax.ppermute(block, axis, route)
 
 
@@ -461,44 +689,28 @@
 
     w = in_proj[0]
     rows = w.shape[0]
-
-    def cut(lo, count):
-        part = w[:, lo : lo + count].reshape(rows, group, count // group)
-        return jnp.swapaxes(part, 0, 1)
-
-    shared = jnp.broadcast_to(w[:, inner:chans][None], (group, rows, 2 * state))
     tail = hs + hs * levels_all
-    used = 2 * wide + 2 * state + tail
-    padded = -(-used // 128) * 128
-    w_parts = jnp.concatenate(
+    lanes = -(-tail // 128) * 128
+    at = chans + inner
+    tails = jnp.concatenate(
         [
-            cut(0, inner),
-            shared,
-            cut(chans, inner),
-            cut(chans + inner, heads),
-            cut(chans + inner + heads, heads * levels_all),
-            jnp.zeros((group, rows, padded - used), w.dtype),
+            w[:, at : at + heads].reshape(rows, group, hs),
+            w[:, at + heads :].reshape(rows, group, hs * levels_all),
         ],
         axis=2,
     )
+    tails = jnp.swapaxes(jnp.pad(tails, ((0, 0), (0, 0), (0, lanes - tail))), 0, 1)
     u = (
         hidden * lax.rsqrt(jnp.mean(hidden * hidden, axis=1, keepdims=True) + EPS) * norm_gain[0]
     ).astype(bf16)
-    u = jnp.swapaxes(u.reshape(length, n // group, group * rows), 0, 1)
-    p = gathered(u, w_parts, n)
+    p, halo = gathered(u, w, tails, n, (wide, inner, chans))
 
     def mine(vector, count):
         return lax.dynamic_slice_in_dim(vector, inner_at * count, count, axis=-1)
 
-    mixed_ch = wide + 2 * state
     dims = (wide, state, head_size, taps)
-    lasts = p[:, length - margin :, :mixed_ch]
-    earlier = from_behind(lasts[group - 1 :], "seq", group)
-    halo = jnp.concatenate([earlier, lasts[: group - 1]], axis=0).astype(f32)
-    halo = jnp.pad(halo, ((0, 0), (-margin % 8, 0), (0, 0)))
     taps_w = jnp.concatenate([mine(conv_weight[0][:, :inner], wide), conv_weight[0][:, inner:]], 1)
     taps_b = jnp.concatenate([mine(conv_bias[0][:inner], wide), conv_bias[0][inner:]], 0)[None]
-    lanes = padded - mixed_ch - wide
     small_bias = jnp.concatenate([mine(dt_bias[0], hs), mine(level_bias[0], hs * levels_all)])
     small_bias = jnp.pad(small_bias, (0, lanes - tail))[None]
     rate = jnp.pad(mine(decay_rate[0], hs), (0, lanes - hs))[None]
@@ -510,8 +722,8 @@
     x, bc, small, cum, states = per_block(
         functools.partial(state_kernel, dims),
         group,
-        (p, halo),
-        (taps_w, taps_b, small_bias, rate),
+        (p,),
+        (halo, taps_w, taps_b, small_bias, rate),
         (
             shaped(bf16, length, wide),
             shaped(bf16, length, 2 * state),
@@ -520,6 +732,7 @@
             shaped(f32, state, wide),
         ),
         2 * tokens * state * wide,
+        16,
     )
     (y,) = per_block(
         functools.partial(inside_kernel, dims, levels_all),
@@ -566,21 +779,15 @@
         before_log = jnp.where(upper, before_log + other_log, before_log)
         block_log = block_log + other_log
     stacked = jnp.stack([jnp.stack(held) for held in buckets]).astype(bf16)
-    (gated,) = per_block(
-        functools.partial(outside_kernel, dims, levels_all, levels_used),
-        group,
+    result = finished(
+        dims,
+        levels_all,
+        levels_used,
         (y, bc, stacked, small, cum, p),
-        (),
-        (shaped(bf16, length, wide),),
-        2 * tokens * state * wide * levels_used,
-    )
-
-    own = exchanged(gated)
-    own = jnp.swapaxes(own, 0, 1).reshape(length, inner).astype(f32)
-    normed = (
-        own * lax.rsqrt(jnp.mean(own * own, axis=1, keepdims=True) + EPS) * gate_gain[0]
-    ).astype(bf16)
-    result = (hidden + jnp.dot(normed, out_proj[0], preferred_element_type=f32)).astype(bf16)
+        acts[0],
+        gate_gain[0].reshape(group, 1, wide),
+        out_proj[0].reshape(group, wide, -1),
+    )
     moved = passed_along(result, "section", 1)
     return moved[None]
 

time: 204 us -> 174 us (0.85)
  local copies, waits for them, and re-layouts: 28.4 us -> 19.1 us
  Pallas kernels: 144 us -> 138 us
  matrix products: 5.73 us -> 0 us
  starting transfers between devices: 7.29 us -> 2.55 us
  other arithmetic: 13.9 us -> 9.32 us
    dot_general x1 -> x0, matrix products: 5.73 us -> none  [per_device(): jnp.dot(normed, out_proj[0], preferred_element_type=f32)]
    pallas_call x3 -> x2, Pallas kernels: 15.5 us -> 10.4 us  [per_block(): pl.pallas_call(kernel, grid=(group,), out_shape=outs, in_specs=specs, out...]
    slice x5 -> x4, local copies, waits for them, and re-layouts: 4.82 us -> 0.3 us  [the longest x2 0.22 us: per_device(): w[:, at + heads:].reshape(rows, group, hs * levels_all)]
    unnamed x46 -> x56, local copies, waits for them, and re-layouts: 9.26 us -> 13.2 us
    ppermute x3, starting transfers between devices: 5.76 us -> 2.48 us  [swapped(): return lax.ppermute(block, axis, route)]
    reshape x5 -> x2, local copies, waits for them, and re-layouts: 3.49 us -> 0.31 us  [the longest x1 0.17 us: per_device(): w[:, at:at + heads].reshape(rows, group, hs)]
    convert_element_type x3 -> x0, local copies, waits for them, and re-layouts: 2.9 us -> none  [the longest x2 2.37 us: per_device(): hidden = acts[0].astype(f32)]
    exp x11, local copies, waits for them, and re-layouts: 3.7 us -> 1.37 us  [faded(): return jnp.exp(jnp.repeat(log, head_size))[None] * block]
  transfers between devices with their start and end apart: 5 -> 4, of which waited for: 1 -> 2; matrix products, arithmetic and copies ran while one was open for 4% -> 3% of each run, Pallas kernels for 2% -> 2%
where the time goes in v3:
time: 174 us; the launch traced here: 173 us
  Pallas kernels  138 us (79%)
  local copies, waits for them, and re-layouts  19.1 us (11%)
  other arithmetic  9.32 us (5%)
  waiting for transfers between devices  3.9 us (2%)
  starting transfers between devices  2.55 us (1%)
    pallas_call x1, Pallas kernels, gathered(): pl.pallas_call(functools.partial(gather_kernel, group, n, starts), out_sh...  109 us
    pallas_call x1, Pallas kernels, finished(): pl.pallas_call(functools.partial(outside_kernel, dims, levels, used, grou...  18.4 us
    unnamed x56, local copies, waits for them, and re-layouts  13.2 us
    pallas_call x2, Pallas kernels, per_block(): pl.pallas_call(kernel, grid=(group,), out_shape=outs, in_specs=specs, out...  10.4 us
    another operation x6, other arithmetic, per_device(): stacked = jnp.stack([jnp.stack(held) for held in buckets]).astype(bf16)  5.46 us
  transfers between devices with their start and end apart: 4, of which 2 were waited for; matrix products, arithmetic and copies ran while one was open for 3% of the time, Pallas kernels for 2%

profile of v3, /device:TPU:0, one launch (start us, length us, event | category | flops | bytes accessed | tf_op | source)
XLA Modules:
  0.0 173.3 jit_solution(2187821955101524522)
XLA Ops:
  1.6 1.7 copy.13
  4.6 1.3 fusion.2.u_ref
  6.7 109.3 %shard_map.109 = (bf16[4,256,1408]{2,1,0:T(8,128)(2,1)}, bf16[16,1408]{1,0:T(8,128)(2,1)}) custom-call(bf16[256,2048]{1,0:T(8,128)(2,1)} %fusion.2.u_ref, bf16[128,4640]{1,0:T(8,128)(2,1)} %bitcast.106, bf16[4,128,128]{2,1,0:T(8,128)(2,1)} %fusion.23.tail_ref), custom_call_target="tpu_custom_call" | custom-call | tf_op jit(solution)/shard_map/pallas_call | solution.py:349
  116.0 1.8 %copy-done.1 = bf16[4,256,1408]{2,1,0:T(8,128)(2,1)S(1)} copy-done((bf16[4,256,1408]{2,1,0:T(8,128)(2,1)S(1)}, bf16[4,256,1408]{2,1,0:T(8,128)(2,1)}, u32[]{:S(2)}) %copy-start.1) | copy-done | bytes 2883608
  117.8 0.8 copy-done.12
  118.6 6.3 %shard_map.110 = (bf16[4,256,512]{2,1,0:T(8,128)(2,1)S(1)}, bf16[4,256,256]{2,1,0:T(8,128)(2,1)S(1)}, f32[4,256,128]{2,1,0:T(8,128)S(1)}, f32[4,256,128]{2,1,0:T(8,128)S(1)}, f32[4,128,512]{2,1,0:T(8,128)S(1)}) custom-call(bf16[4,256,1408]{2,1,0:T(8,128)(2,1)S(1)} %copy-done.1, bf16[4,256,1408]{2,1,0:T(8,128)(2,1)S(1)} %copy-done.1, ...), custom_call_target="tpu_custom_call" | custom-call | flops 134217728 | bytes 5828608 | tf_op jit(solution)/shard_map/pallas_call | solution.py:592
  124.9 0.8 copy-done.6
  125.7 0.8 copy-done.9
  126.5 1.0 copy-done.14
  127.5 2.4 %collective-permute-start.1 = (f32[8]{0:T(128)S(1)}, f32[8]{0:T(128)S(1)}, u32[]{:S(2)}, u32[]{:S(2)}) collective-permute-start(f32[8]{0:T(128)S(1)} %get-tuple-element.20), channel_id=1, source_target_pairs={{0,4},{4,0},{1,5},{5,1},{2,6},{6,2},{3,7},{7,3},{8,12},{12,8},{9,1... | collective-permute-start | bytes 104 | tf_op jit(solution)/shard_map/ppermute | solution.py:648
  129.9 0.8 copy-done.3
  135.1 1.2 collective-permute-done
  136.3 0.9 fusion.27
  137.2 1.0 copy-done.4
  138.3 1.0 copy-done.7
  139.3 1.0 copy-done.10
  140.3 1.2 copy-done.15
  141.6 4.1 %shard_map.111.y_ref = f32[4,256,512]{2,1,0:T(8,128)S(1)} custom-call(bf16[4,256,512]{2,1,0:T(8,128)(2,1)S(1)} %copy-done.15, bf16[4,256,256]{2,1,0:T(8,128)(2,1)S(1)} %copy-done.7, f32[4,256,128]{2,1,0:T(8,128)S(1)} %copy-done.10, f32[4,256,128]{2,1,0:T(8,128)S(1)} %copy-done.4, f32[1,512]{1,0:T(1,128)S(1)} %broadcast_in_dim_reshape.3.skip_ref), custom_call_target="tpu_custom_call" | custom-call | flops 2147483648 | bytes 2623488 | tf_op jit(solution)/shard_map/pallas_call | solution.py:592
  146.5 1.1 fusion.18
  148.3 1.0 maximum_bitcast_fusion.3
  149.5 1.6 pad_maximum_fusion.bucket_ref
  151.2 18.4 %shard_map.112 = bf16[256,2048]{1,0:T(8,128)(2,1)S(1)} custom-call(f32[4,256,512]{2,1,0:T(8,128)S(1)} %shard_map.111.y_ref, bf16[4,256,256]{2,1,0:T(8,128)(2,1)S(1)} %copy-done.8, bf16[4,4,128,512]{3,2,1,0:T(8,128)(2,1)} %pad_maximum_fusion.bucket_ref, f32[4,256,128]{2,1,0:T(8,128)S(1)} %copy-done.11, f32[4,256,128]{2,1,0:T(8,128)S(1)} %copy-done.5, ...), custom_call_target="tpu_custom_call" | custom-call | tf_op jit(solution)/shard_map/pallas_call | solution.py:550
  169.7 2.6 %collective-permute-done.3 = bf16[256,2048]{1,0:T(8,128)(2,1)S(1)} collective-permute-done((bf16[256,2048]{1,0:T(8,128)(2,1)S(1)}, bf16[256,2048]{1,0:T(8,128)(2,1)S(1)}, u32[]{:S(2)}, u32[]{:S(2)}) %collective-permute-start.3) | collective-permute-done | bytes 1048608 | tf_op jit(solution)/shard_map/ppermute | solution.py:654
  172.3 1.0 copy.19
  (107 shorter events, 9.7 us)
Async XLA Ops:
  0.0 4.5 %copy-start = (f32[1,256]{1,0:T(1,128)S(1)}, f32[1,256]{1,0:T(1,128)}, u32[]{:S(2)}) copy-start(f32[1,256]{1,0:T(1,128)} %param.19) | copy-start | bytes 3076
  0.0 3.9 %slice-start.1 = ((f32[1,2304]{1,0:T(1,128)}), f32[1,2048]{1,0:T(1,128)S(1)}, s32[]{:S(2)}) async-start(f32[1,2304]{1,0:T(1,128)} %param.15), calls=%async_computation.1 | async-start | bytes 16384 | tf_op jit(solution)/shard_map/slice | solution.py:713
  0.0 3.9 %slice-start = ((f32[1,2304]{1,0:T(1,128)}), f32[1,256]{1,0:T(1,128)S(1)}, s32[]{:S(2)}) async-start(f32[1,2304]{1,0:T(1,128)} %param.15), calls=%async_computation | async-start | bytes 2048 | tf_op jit(solution)/shard_map/slice | solution.py:713
  0.0 3.4 %copy-start.25 = (f32[1,32]{1,0:T(1,128)S(1)}, f32[1,32]{1,0:T(1,128)}, u32[]{:S(2)}) copy-start(f32[1,32]{1,0:T(1,128)} %param.17) | copy-start | bytes 388
  0.0 3.4 %copy-start.24 = (f32[1,32]{1,0:T(1,128)S(1)}, f32[1,32]{1,0:T(1,128)}, u32[]{:S(2)}) copy-start(f32[1,32]{1,0:T(1,128)} %param.16) | copy-start | bytes 388
  0.0 3.5 %copy-start.2 = (bf16[1,256,2048]{2,1,0:T(8,128)(2,1)S(1)}, bf16[1,256,2048]{2,1,0:T(8,128)(2,1)}, u32[]{:S(2)}) copy-start(bf16[1,256,2048]{2,1,0:T(8,128)(2,1)} %param.11) | copy-start | bytes 3145732
  1.6 3.1 %copy-start.22 = (f32[1,2048]{1,0:T(1,128)S(1)}, f32[1,2048]{1,0:T(1,128)}, u32[]{:S(2)}) copy-start(f32[1,2048]{1,0:T(1,128)} %param.20) | copy-start | bytes 24580
  3.3 3.4 %copy-start.16 = (bf16[1,128,4640]{2,1,0:T(8,128)(2,1)}, bf16[1,128,4640]{2,1,0:T(8,128)(2,1)S(1)}, u32[]{:S(2)}) copy-start(bf16[1,128,4640]{2,1,0:T(8,128)(2,1)S(1)} %copy.13) | copy-start | bytes 3563524
  116.0 1.8 %copy-start.1 = (bf16[4,256,1408]{2,1,0:T(8,128)(2,1)S(1)}, bf16[4,256,1408]{2,1,0:T(8,128)(2,1)}, u32[]{:S(2)}) copy-start(bf16[4,256,1408]{2,1,0:T(8,128)(2,1)} %get-tuple-element.12.p_ref.before_ref) | copy-start | bytes 8650756
  118.6 13.5 %copy-start.26 = (f32[1,32]{1,0:T(1,128)S(1)}, f32[1,32]{1,0:T(1,128)}, u32[]{:S(2)}) copy-start(f32[1,32]{1,0:T(1,128)} %param.18) | copy-start | bytes 388
  127.5 6.8 %collective-permute-start.1 = (f32[8]{0:T(128)S(1)}, f32[8]{0:T(128)S(1)}, u32[]{:S(2)}, u32[]{:S(2)}) collective-permute-start(f32[8]{0:T(128)S(1)} %get-tuple-element.20), channel_id=1, source_target_pairs={{0,4},{4,0},{1,5},{5,1},{2,6},{6,2},{3,7},{7,3},{8,12},{12,8},{9,1... | collective-permute-start | bytes 104 | tf_op jit(solution)/shard_map/ppermute | solution.py:648
  131.3 5.0 %collective-permute-start = (bf16[128,512]{1,0:T(8,128)(2,1)S(1)}, bf16[128,512]{1,0:T(8,128)(2,1)S(1)}, u32[]{:S(2)}, u32[]{:S(2)}) collective-permute-start(bf16[128,512]{1,0:T(8,128)(2,1)S(1)} %get-tuple-element.21), channel_id=1, source_target_pairs={{0,4},{4,0},{1,5},{5,1},{2,6},{6,2},{3,7},{7,3},{8,12},{12,8},{9,1... | collective-permute-start | bytes 393224 | tf_op jit(solution)/shard_map/ppermute | solution.py:648
  133.0 4.2 %copy-start.21 = (f32[512]{0:T(512)}, f32[512]{0:T(512)S(1)}, u32[]{:S(2)}) copy-start(f32[512]{0:T(512)S(1)} %exp.140) | copy-start | bytes 6148
  137.2 9.2 %collective-permute-start.2 = (bf16[128,512]{1,0:T(8,128)(2,1)}, bf16[128,512]{1,0:T(8,128)(2,1)}, u32[]{:S(2)}, u32[]{:S(2)}) collective-permute-start(bf16[128,512]{1,0:T(8,128)(2,1)} %get-tuple-element.41), channel_id=1, source_target_pairs={{0,8},{8,0},{1,9},{9,1},{2,10},{10,2},{3,11},{11,3},{4,12},{12,4},... | collective-permute-start | bytes 393224 | tf_op jit(solution)/shard_map/ppermute | solution.py:648
  141.6 4.1 %copy-start.23 = (f32[8]{0:T(128)S(1)}, f32[8]{0:T(128)}, u32[]{:S(2)}) copy-start(f32[8]{0:T(128)} %get-tuple-element.45) | copy-start | bytes 100
  146.4 2.9 %copy-start.17 = (bf16[1,128,512]{2,1,0:T(8,128)(2,1)S(1)}, bf16[1,128,512]{2,1,0:T(8,128)(2,1)}, u32[]{:S(2)}) copy-start(bf16[1,128,512]{2,1,0:T(8,128)(2,1)} %get-tuple-element.25) | copy-start | bytes 393220
  146.4 2.9 %copy-start.18 = (bf16[1,128,512]{2,1,0:T(8,128)(2,1)S(1)}, bf16[1,128,512]{2,1,0:T(8,128)(2,1)}, u32[]{:S(2)}) copy-start(bf16[1,128,512]{2,1,0:T(8,128)(2,1)} %get-tuple-element.23) | copy-start | bytes 393220
  146.4 2.9 %copy-start.19 = (bf16[1,128,512]{2,1,0:T(8,128)(2,1)S(1)}, bf16[1,128,512]{2,1,0:T(8,128)(2,1)}, u32[]{:S(2)}) copy-start(bf16[1,128,512]{2,1,0:T(8,128)(2,1)} %get-tuple-element.39) | copy-start | bytes 393220
  146.4 2.9 %copy-start.20 = (bf16[1,128,512]{2,1,0:T(8,128)(2,1)S(1)}, bf16[1,128,512]{2,1,0:T(8,128)(2,1)}, u32[]{:S(2)}) copy-start(bf16[1,128,512]{2,1,0:T(8,128)(2,1)} %get-tuple-element.42) | copy-start | bytes 393220
  149.5 1.7 copy-start.5
  149.5 1.7 copy-start.8
  149.5 1.7 copy-start.11
  149.5 1.7 copy-start.13
  169.6 2.7 %collective-permute-start.3 = (bf16[256,2048]{1,0:T(8,128)(2,1)S(1)}, bf16[256,2048]{1,0:T(8,128)(2,1)S(1)}, u32[]{:S(2)}, u32[]{:S(2)}) collective-permute-start(bf16[256,2048]{1,0:T(8,128)(2,1)S(1)} %shard_map.112), channel_id=1, source_target_pairs={{0,16},{16,0},{1,17},{17,1},{2,18},{18,2},{3,19},{19,3},{4,20},{20... | collective-permute-start | bytes 3145736 | tf_op jit(solution)/shard_map/ppermute | solution.py:654
  (9 other events, 8.6 us)

commit v4 on v3

--- a/solution.py
+++ b/solution.py
@@ -28,6 +28,12 @@
     pl.semaphore_signal(
         pltpu.get_barrier_semaphore(), inc=1, device_id={"seq": seq}, device_id_type=MESH
     )
+
+
+def partner(inner, step, group):
+    low = lax.rem(lax.rem(inner, 2) + step % 2, 2)
+    high = lax.rem(inner // 2 + step // 2, max(group // 2, 1))
+    return high * 2 + low
 
 
 def gather_kernel(
@@ -51,7 +57,7 @@
     has_down = outer > 0
     barrier = pltpu.get_barrier_semaphore()
     for step in range(1, group):
-        greet(base + lax.rem(inner + step, group))
+        greet(base + partner(inner, step, group))
 
     @pl.when(has_up)
     def _():
@@ -103,7 +109,7 @@
 
     def across(source, step):
         piece = bc_slot(source, inner)
-        peer = base + lax.rem(inner + step, group)
+        peer = base + partner(inner, step, group)
         at = source * group
         return remote(piece, piece, bc_peer.at[at + step], bc_recv.at[at + inner], peer)
 
@@ -120,12 +126,15 @@
     pltpu.make_async_copy(bc_src, bc_slot(outer, inner), own_sem.at[0]).start()
     own_u = pltpu.make_async_copy(u_ref, u_all.at[inner], own_sem.at[1])
     own_u.start()
-    for step in range(1, group):
-        peer = lax.rem(inner + step, group)
+    def give(step):
+        peer = partner(inner, step, group)
         for src, lo, hi in parts_for(peer):
             remote(
                 src, slot_at(outer, inner, lo, hi), w_send.at[step], w_recv.at[me], base + peer
             ).start()
+
+    for step in range(1, min(group, 3)):
+        give(step)
     whole_slot = slot_at(outer, inner, 0, columns)
     pltpu.make_async_copy(whole_slot, whole_slot, own_sem.at[0]).wait()
 
@@ -140,8 +149,11 @@
         along(outer, -1).start()
 
     for step in range(1, group):
-        slot = lax.rem(inner + step, group)
+        slot = partner(inner, step, group)
         arrived(outer, slot)
+        if step == 1:
+            for far in range(3, group):
+                give(far)
 
         @pl.when(has_up)
         def _():
@@ -153,7 +165,7 @@
 
     sends = []
     for step in range(1, group):
-        peer = lax.rem(inner + step, group)
+        peer = partner(inner, step, group)
         copy = remote(u_ref, u_all.at[inner], u_send.at[step], u_recv.at[inner], base + peer)
         copy.start()
         sends.append(copy)
@@ -176,7 +188,7 @@
 
     def ready(source):
         for step in range(1, group):
-            bc_arrived(source, lax.rem(inner + step, group))
+            bc_arrived(source, partner(inner, step, group))
 
     def multiply_both(distance, block):
         @pl.when(outer - distance >= 0)
@@ -196,7 +208,7 @@
             multiply(outer + distance, block)
 
     def relay(distance, block):
-        slot = lax.rem(inner + block, group)
+        slot = partner(inner, block, group)
 
         @pl.when(outer - distance >= 0)
         def _():
@@ -242,16 +254,24 @@
         relay(1, block)
         return carry
 
+    def relay_second(block, carry):
+        relay(2, block)
+        return carry
+
     if outers > 1:
         lax.fori_loop(0, group, relay_first, 0)
+    if outers > 2:
+        lax.fori_loop(0, group, relay_second, 0)
     own_u.wait()
     for step in range(1, group):
-        peer = lax.rem(inner + step, group)
+        peer = partner(inner, step, group)
         remote(u_all.at[peer], u_all.at[peer], u_send.at[0], u_recv.at[peer], me).wait_recv()
     ready(outer)
 
     def own_work(block, carry):
         multiply(outer, block, True)
+        if outers > 2:
+            multiply_both(1, block)
         return carry
 
     lax.fori_loop(0, group, own_work, 0)
@@ -263,7 +283,7 @@
         multiply_both(distance - 1, block)
         return carry
 
-    lax.fori_loop(2 * group, outers * group, later, 0)
+    lax.fori_loop(3 * group, max(outers, 3) * group, later, 0)
 
     def finish(step, carry):
         if outers > 1:
@@ -486,17 +506,17 @@
     load = pltpu.make_async_copy(w_hbm, w_ref, w_sem)
     load.start()
     for step in range(1, group):
-        greet(base + lax.rem(inner + step, group))
+        greet(base + partner(inner, group - step, group))
     pl.semaphore_wait(pltpu.get_barrier_semaphore(), group - 1)
 
     def copy_to(step):
-        peer = lax.rem(inner + step, group)
+        peer = partner(inner, group - step, group)
         return remote(
             q_own.at[peer], q_got.at[inner], send_sem.at[step], recv_sem.at[inner], base + peer
         )
 
     def work(step, carry):
-        block = lax.rem(inner + step, group)
+        block = partner(inner, group - step, group)
         c = bc_ref[block, :, state:]
         small = small_ref[block]
         total = None
@@ -529,7 +549,7 @@
     acc[...], squares = project(q_own[inner], inner)
 
     def add(step, squares):
-        peer = lax.rem(inner + step, group)
+        peer = partner(inner, group - step, group)
         remote(q_got.at[peer], q_got.at[peer], send_sem.at[0], recv_sem.at[peer], me).wait_recv()
         part, more = project(q_got[peer], peer)
         acc[...] += part

time: 174 us -> 160 us (0.920)
  Pallas kernels: 138 us -> 124 us
    pallas_call x1, Pallas kernels: 109 us -> 95.8 us  [gathered(): pl.pallas_call(functools.partial(gather_kernel, group, n, starts), out_sh...]
  transfers between devices with their start and end apart: 4 -> 4, of which waited for: 2 -> 2; matrix products, arithmetic and copies ran while one was open for 3% -> 3% of each run, Pallas kernels for 2% -> 3%
where the time goes in v4:
time: 160 us
  Pallas kernels  124 us (78%)
  local copies, waits for them, and re-layouts  19.1 us (12%)
  other arithmetic  9.32 us (6%)
  waiting for transfers between devices  3.9 us (2%)
  starting transfers between devices  2.55 us (2%)
    pallas_call x1, Pallas kernels, gathered(): pl.pallas_call(functools.partial(gather_kernel, group, n, starts), out_sh...  95.8 us
    pallas_call x1, Pallas kernels, finished(): pl.pallas_call(functools.partial(outside_kernel, dims, levels, used, grou...  18.3 us
    unnamed x56, local copies, waits for them, and re-layouts  13.2 us
    pallas_call x2, Pallas kernels, per_block(): pl.pallas_call(kernel, grid=(group,), out_shape=outs, in_specs=specs, out...  10.4 us
    another operation x6, other arithmetic, per_device(): stacked = jnp.stack([jnp.stack(held) for held in buckets]).astype(bf16)  5.46 us
  transfers between devices with their start and end apart: 4, of which 2 were waited for; matrix products, arithmetic and copies ran while one was open for 3% of the time, Pallas kernels for 3%

profile of v4, /device:TPU:0, one launch (start us, length us, event | category | flops | bytes accessed | tf_op | source)
XLA Modules:
  0.0 159.7 jit_solution(2437222683368377727)
XLA Ops:
  1.6 1.7 %copy.13 = bf16[1,128,4640]{2,1,0:T(8,128)(2,1)S(1)} copy(bf16[1,128,4640]{1,2,0:T(8,128)(2,1)} %param.12) | data formatting | bytes 2375680 | tf_op args[1]
  4.6 1.3 fusion.2.u_ref
  6.7 95.8 %shard_map.109 = (bf16[4,256,1408]{2,1,0:T(8,128)(2,1)}, bf16[16,1408]{1,0:T(8,128)(2,1)}) custom-call(bf16[256,2048]{1,0:T(8,128)(2,1)} %fusion.2.u_ref, bf16[128,4640]{1,0:T(8,128)(2,1)} %bitcast.106, bf16[4,128,128]{2,1,0:T(8,128)(2,1)} %fusion.23.tail_ref), custom_call_target="tpu_custom_call" | custom-call | tf_op jit(solution)/shard_map/pallas_call | solution.py:369
  102.5 1.8 %copy-done.1 = bf16[4,256,1408]{2,1,0:T(8,128)(2,1)S(1)} copy-done((bf16[4,256,1408]{2,1,0:T(8,128)(2,1)S(1)}, bf16[4,256,1408]{2,1,0:T(8,128)(2,1)}, u32[]{:S(2)}) %copy-start.1) | copy-done | bytes 2883608
  104.3 0.8 copy-done.12
  105.1 6.3 %shard_map.110 = (bf16[4,256,512]{2,1,0:T(8,128)(2,1)S(1)}, bf16[4,256,256]{2,1,0:T(8,128)(2,1)S(1)}, f32[4,256,128]{2,1,0:T(8,128)S(1)}, f32[4,256,128]{2,1,0:T(8,128)S(1)}, f32[4,128,512]{2,1,0:T(8,128)S(1)}) custom-call(bf16[4,256,1408]{2,1,0:T(8,128)(2,1)S(1)} %copy-done.1, bf16[4,256,1408]{2,1,0:T(8,128)(2,1)S(1)} %copy-done.1, ...), custom_call_target="tpu_custom_call" | custom-call | flops 134217728 | bytes 5828608 | tf_op jit(solution)/shard_map/pallas_call | solution.py:612
  111.4 0.8 copy-done.6
  112.2 0.8 copy-done.9
  113.0 1.0 copy-done.14
  114.0 2.4 %collective-permute-start.1 = (f32[8]{0:T(128)S(1)}, f32[8]{0:T(128)S(1)}, u32[]{:S(2)}, u32[]{:S(2)}) collective-permute-start(f32[8]{0:T(128)S(1)} %get-tuple-element.20), channel_id=1, source_target_pairs={{0,4},{4,0},{1,5},{5,1},{2,6},{6,2},{3,7},{7,3},{8,12},{12,8},{9,1... | collective-permute-start | bytes 104 | tf_op jit(solution)/shard_map/ppermute | solution.py:668
  116.4 0.8 copy-done.3
  121.5 1.2 collective-permute-done
  122.8 0.9 fusion.27
  123.7 1.0 copy-done.4
  124.7 1.0 copy-done.7
  125.8 1.0 copy-done.10
  126.8 1.2 copy-done.15
  128.1 4.1 %shard_map.111.y_ref = f32[4,256,512]{2,1,0:T(8,128)S(1)} custom-call(bf16[4,256,512]{2,1,0:T(8,128)(2,1)S(1)} %copy-done.15, bf16[4,256,256]{2,1,0:T(8,128)(2,1)S(1)} %copy-done.7, f32[4,256,128]{2,1,0:T(8,128)S(1)} %copy-done.10, f32[4,256,128]{2,1,0:T(8,128)S(1)} %copy-done.4, f32[1,512]{1,0:T(1,128)S(1)} %broadcast_in_dim_reshape.3.skip_ref), custom_call_target="tpu_custom_call" | custom-call | flops 2147483648 | bytes 2623488 | tf_op jit(solution)/shard_map/pallas_call | solution.py:612
  132.9 1.1 fusion.18
  134.8 1.0 maximum_bitcast_fusion.3
  136.0 1.6 %pad_maximum_fusion.bucket_ref = bf16[4,4,128,512]{3,2,1,0:T(8,128)(2,1)} fusion(bf16[1,4,128,512]{3,2,1,0:T(8,128)(2,1)S(1)} %maximum_bitcast_fusion.3, bf16[1,4,128,512]{3,2,1,0:T(8,128)(2,1)S(1)} %get-tuple-element.44, bf16[1,4,128,512]{3,2,1,0:T(8,128)(2,1)S(1)} %get-tuple-element.43, bf16[1,4,128,512]{3,2,1,0:T(8,128)(2,1)S(1)} %maximum_bitcast_fusion), kind=kLoop, calls=%fused_computation.5 | loop fusion | flops 3145728 | bytes 4194304 | tf_op jit(solution)/shard_map/stack | solution.py:801
  137.7 18.3 %shard_map.112 = bf16[256,2048]{1,0:T(8,128)(2,1)S(1)} custom-call(f32[4,256,512]{2,1,0:T(8,128)S(1)} %shard_map.111.y_ref, bf16[4,256,256]{2,1,0:T(8,128)(2,1)S(1)} %copy-done.8, bf16[4,4,128,512]{3,2,1,0:T(8,128)(2,1)} %pad_maximum_fusion.bucket_ref, f32[4,256,128]{2,1,0:T(8,128)S(1)} %copy-done.11, f32[4,256,128]{2,1,0:T(8,128)S(1)} %copy-done.5, ...), custom_call_target="tpu_custom_call" | custom-call | tf_op jit(solution)/shard_map/pallas_call | solution.py:570
  156.1 2.6 %collective-permute-done.3 = bf16[256,2048]{1,0:T(8,128)(2,1)S(1)} collective-permute-done((bf16[256,2048]{1,0:T(8,128)(2,1)S(1)}, bf16[256,2048]{1,0:T(8,128)(2,1)S(1)}, u32[]{:S(2)}, u32[]{:S(2)}) %collective-permute-start.3) | collective-permute-done | bytes 1048608 | tf_op jit(solution)/shard_map/ppermute | solution.py:674
  158.7 1.0 copy.19
  (107 shorter events, 9.7 us)
Async XLA Ops:
  0.0 4.5 %copy-start = (f32[1,256]{1,0:T(1,128)S(1)}, f32[1,256]{1,0:T(1,128)}, u32[]{:S(2)}) copy-start(f32[1,256]{1,0:T(1,128)} %param.19) | copy-start | bytes 3076
  0.0 3.9 %slice-start.1 = ((f32[1,2304]{1,0:T(1,128)}), f32[1,2048]{1,0:T(1,128)S(1)}, s32[]{:S(2)}) async-start(f32[1,2304]{1,0:T(1,128)} %param.15), calls=%async_computation.1 | async-start | bytes 16384 | tf_op jit(solution)/shard_map/slice | solution.py:733
  0.0 3.9 %slice-start = ((f32[1,2304]{1,0:T(1,128)}), f32[1,256]{1,0:T(1,128)S(1)}, s32[]{:S(2)}) async-start(f32[1,2304]{1,0:T(1,128)} %param.15), calls=%async_computation | async-start | bytes 2048 | tf_op jit(solution)/shard_map/slice | solution.py:733
  0.0 3.4 %copy-start.25 = (f32[1,32]{1,0:T(1,128)S(1)}, f32[1,32]{1,0:T(1,128)}, u32[]{:S(2)}) copy-start(f32[1,32]{1,0:T(1,128)} %param.17) | copy-start | bytes 388
  0.0 3.4 %copy-start.24 = (f32[1,32]{1,0:T(1,128)S(1)}, f32[1,32]{1,0:T(1,128)}, u32[]{:S(2)}) copy-start(f32[1,32]{1,0:T(1,128)} %param.16) | copy-start | bytes 388
  0.0 3.5 %copy-start.2 = (bf16[1,256,2048]{2,1,0:T(8,128)(2,1)S(1)}, bf16[1,256,2048]{2,1,0:T(8,128)(2,1)}, u32[]{:S(2)}) copy-start(bf16[1,256,2048]{2,1,0:T(8,128)(2,1)} %param.11) | copy-start | bytes 3145732
  1.6 3.1 %copy-start.22 = (f32[1,2048]{1,0:T(1,128)S(1)}, f32[1,2048]{1,0:T(1,128)}, u32[]{:S(2)}) copy-start(f32[1,2048]{1,0:T(1,128)} %param.20) | copy-start | bytes 24580
  3.3 3.4 %copy-start.16 = (bf16[1,128,4640]{2,1,0:T(8,128)(2,1)}, bf16[1,128,4640]{2,1,0:T(8,128)(2,1)S(1)}, u32[]{:S(2)}) copy-start(bf16[1,128,4640]{2,1,0:T(8,128)(2,1)S(1)} %copy.13) | copy-start | bytes 3563524
  102.5 1.8 %copy-start.1 = (bf16[4,256,1408]{2,1,0:T(8,128)(2,1)S(1)}, bf16[4,256,1408]{2,1,0:T(8,128)(2,1)}, u32[]{:S(2)}) copy-start(bf16[4,256,1408]{2,1,0:T(8,128)(2,1)} %get-tuple-element.12.p_ref.before_ref) | copy-start | bytes 8650756
  105.1 13.5 %copy-start.26 = (f32[1,32]{1,0:T(1,128)S(1)}, f32[1,32]{1,0:T(1,128)}, u32[]{:S(2)}) copy-start(f32[1,32]{1,0:T(1,128)} %param.18) | copy-start | bytes 388
  114.0 6.8 %collective-permute-start.1 = (f32[8]{0:T(128)S(1)}, f32[8]{0:T(128)S(1)}, u32[]{:S(2)}, u32[]{:S(2)}) collective-permute-start(f32[8]{0:T(128)S(1)} %get-tuple-element.20), channel_id=1, source_target_pairs={{0,4},{4,0},{1,5},{5,1},{2,6},{6,2},{3,7},{7,3},{8,12},{12,8},{9,1... | collective-permute-start | bytes 104 | tf_op jit(solution)/shard_map/ppermute | solution.py:668
  117.8 5.0 %collective-permute-start = (bf16[128,512]{1,0:T(8,128)(2,1)S(1)}, bf16[128,512]{1,0:T(8,128)(2,1)S(1)}, u32[]{:S(2)}, u32[]{:S(2)}) collective-permute-start(bf16[128,512]{1,0:T(8,128)(2,1)S(1)} %get-tuple-element.21), channel_id=1, source_target_pairs={{0,4},{4,0},{1,5},{5,1},{2,6},{6,2},{3,7},{7,3},{8,12},{12,8},{9,1... | collective-permute-start | bytes 393224 | tf_op jit(solution)/shard_map/ppermute | solution.py:668
  119.5 4.2 %copy-start.21 = (f32[512]{0:T(512)}, f32[512]{0:T(512)S(1)}, u32[]{:S(2)}) copy-start(f32[512]{0:T(512)S(1)} %exp.140) | copy-start | bytes 6148
  123.7 9.2 %collective-permute-start.2 = (bf16[128,512]{1,0:T(8,128)(2,1)}, bf16[128,512]{1,0:T(8,128)(2,1)}, u32[]{:S(2)}, u32[]{:S(2)}) collective-permute-start(bf16[128,512]{1,0:T(8,128)(2,1)} %get-tuple-element.41), channel_id=1, source_target_pairs={{0,8},{8,0},{1,9},{9,1},{2,10},{10,2},{3,11},{11,3},{4,12},{12,4},... | collective-permute-start | bytes 393224 | tf_op jit(solution)/shard_map/ppermute | solution.py:668
  128.0 4.1 %copy-start.23 = (f32[8]{0:T(128)S(1)}, f32[8]{0:T(128)}, u32[]{:S(2)}) copy-start(f32[8]{0:T(128)} %get-tuple-element.45) | copy-start | bytes 100
  132.9 2.9 %copy-start.17 = (bf16[1,128,512]{2,1,0:T(8,128)(2,1)S(1)}, bf16[1,128,512]{2,1,0:T(8,128)(2,1)}, u32[]{:S(2)}) copy-start(bf16[1,128,512]{2,1,0:T(8,128)(2,1)} %get-tuple-element.25) | copy-start | bytes 393220
  132.9 2.9 %copy-start.18 = (bf16[1,128,512]{2,1,0:T(8,128)(2,1)S(1)}, bf16[1,128,512]{2,1,0:T(8,128)(2,1)}, u32[]{:S(2)}) copy-start(bf16[1,128,512]{2,1,0:T(8,128)(2,1)} %get-tuple-element.23) | copy-start | bytes 393220
  132.9 2.9 %copy-start.19 = (bf16[1,128,512]{2,1,0:T(8,128)(2,1)S(1)}, bf16[1,128,512]{2,1,0:T(8,128)(2,1)}, u32[]{:S(2)}) copy-start(bf16[1,128,512]{2,1,0:T(8,128)(2,1)} %get-tuple-element.39) | copy-start | bytes 393220
  132.9 2.9 %copy-start.20 = (bf16[1,128,512]{2,1,0:T(8,128)(2,1)S(1)}, bf16[1,128,512]{2,1,0:T(8,128)(2,1)}, u32[]{:S(2)}) copy-start(bf16[1,128,512]{2,1,0:T(8,128)(2,1)} %get-tuple-element.42) | copy-start | bytes 393220
  136.0 1.7 %copy-start.5 = (f32[4,256,128]{2,1,0:T(8,128)S(1)}, f32[4,256,128]{2,1,0:T(8,128)}, u32[]{:S(2)}) copy-start(f32[4,256,128]{2,1,0:T(8,128)} %copy-done.3) | copy-start | bytes 1572868
  136.0 1.7 %copy-start.8 = (bf16[4,256,256]{2,1,0:T(8,128)(2,1)S(1)}, bf16[4,256,256]{2,1,0:T(8,128)(2,1)}, u32[]{:S(2)}) copy-start(bf16[4,256,256]{2,1,0:T(8,128)(2,1)} %copy-done.6) | copy-start | bytes 1572868
  136.0 1.7 %copy-start.11 = (f32[4,256,128]{2,1,0:T(8,128)S(1)}, f32[4,256,128]{2,1,0:T(8,128)}, u32[]{:S(2)}) copy-start(f32[4,256,128]{2,1,0:T(8,128)} %copy-done.9) | copy-start | bytes 1572868
  136.0 1.7 %copy-start.13 = (f32[1,2048]{1,0:T(1,128)S(1)}, f32[1,2048]{1,0:T(1,128)}, u32[]{:S(2)}) copy-start(f32[1,2048]{1,0:T(1,128)} %param.21) | copy-start | bytes 24580
  156.0 2.7 %collective-permute-start.3 = (bf16[256,2048]{1,0:T(8,128)(2,1)S(1)}, bf16[256,2048]{1,0:T(8,128)(2,1)S(1)}, u32[]{:S(2)}, u32[]{:S(2)}) collective-permute-start(bf16[256,2048]{1,0:T(8,128)(2,1)S(1)} %shard_map.112), channel_id=1, source_target_pairs={{0,16},{16,0},{1,17},{17,1},{2,18},{18,2},{3,19},{19,3},{4,20},{20... | collective-permute-start | bytes 3145736 | tf_op jit(solution)/shard_map/ppermute | solution.py:674
  (9 other events, 8.6 us)

commit v5 on v4

--- a/solution.py
+++ b/solution.py
@@ -494,7 +494,7 @@
 
 
 def outside_kernel(
-    dims, levels, used, group, y_ref, bc_ref, bucket_ref, small_ref, cum_ref, p_ref, acts_ref, gain_ref, w_hbm,
+    dims, levels, used, group, y_ref, bc_ref, near_ref, far_ref, fade_ref, small_ref, cum_ref, p_ref, acts_ref, gain_ref, w_hbm,
     out_ref, q_own, q_got, w_ref, acc, w_sem, send_sem, recv_sem
 ):
     wide, state, size, _ = dims
@@ -519,11 +519,21 @@
         block = partner(inner, group - step, group)
         c = bc_ref[block, :, state:]
         small = small_ref[block]
+        near = near_ref.shape[1]
+
+        def term(level, bucket):
+            reads = jnp.dot(c, bucket, preferred_element_type=f32)
+            return reads * spread(small, selector(lanes, wide, size, hs + level + 1, levels))
+
         total = None
-        for level in range(used):
-            reads = jnp.dot(c, bucket_ref[block, level], preferred_element_type=f32)
-            term = reads * spread(small, selector(lanes, wide, size, hs + level + 1, levels))
-            total = term if total is None else total + term
+        for level in range(near, used):
+            part = term(level, far_ref[level - near])
+            total = part if total is None else total + part
+        if total is not None:
+            total = total * fade_ref[block]
+        for level in range(near):
+            part = term(level, near_ref[block, level])
+            total = part if total is None else total + part
         y = y_ref[block]
         if total is not None:
             y = y + total * spread(jnp.exp(cum_ref[block]), selector(lanes, wide, size, 0, 1))
@@ -570,7 +580,7 @@
     return pl.pallas_call(
         functools.partial(outside_kernel, dims, levels, used, group),
         out_shape=jax.ShapeDtypeStruct((length, width), bf16),
-        in_specs=[vmem] * 8 + [pl.BlockSpec(memory_space=pl.ANY)],
+        in_specs=[vmem] * 10 + [pl.BlockSpec(memory_space=pl.ANY)],
         out_specs=vmem,
         scratch_shapes=[
             pltpu.VMEM((group, length, wide), bf16),
@@ -786,24 +796,26 @@
         summed, logs = merged, merged_logs
     block_state, block_log = summed[0], logs[0]
     before_log = jnp.zeros_like(block_log)
+    far = []
     for bit in range(bits, levels_used):
         other_log, other_state = swapped((block_log, block_state.astype(bf16)), "seq", bit)
         other_state = other_state.astype(f32)
         upper = position >> bit & 1 == 1
         bucket = jnp.where(upper, faded(before_log, other_state), 0.0)
-        for b in range(group):
-            buckets[b].append(faded(before[b], bucket))
+        far.append(bucket.astype(bf16))
         merged_upper = faded(block_log, other_state) + block_state
         merged_lower = faded(other_log, block_state) + other_state
         block_state = jnp.where(upper, merged_upper, merged_lower)
         before_log = jnp.where(upper, before_log + other_log, before_log)
         block_log = block_log + other_log
-    stacked = jnp.stack([jnp.stack(held) for held in buckets]).astype(bf16)
+    near = jnp.stack([jnp.stack(held) for held in buckets]).astype(bf16)
+    far = jnp.stack(far)
+    fade = jnp.exp(jnp.repeat(jnp.stack(before), head_size, axis=1))[:, None]
     result = finished(
         dims,
         levels_all,
         levels_used,
-        (y, bc, stacked, small, cum, p),
+        (y, bc, near, far, fade, small, cum, p),
         acts[0],
         gate_gain[0].reshape(group, 1, wide),
         out_proj[0].reshape(group, wide, -1),

time: 160 us -> 163 us (1.019)
  Pallas kernels: 124 us -> 126 us
  other arithmetic: 9.32 us -> 11.2 us
    another operation x7, other arithmetic: 6.17 us -> 4.28 us  [the longest x3 2.61 us: per_device(): far = jnp.stack(far)]
    unnamed x56 -> x36, local copies, waits for them, and re-layouts: 13.2 us -> 11.8 us
  transfers between devices with their start and end apart: 4 -> 4, of which waited for: 2 -> 1; matrix products, arithmetic and copies ran while one was open for 3% -> 7% of each run, Pallas kernels for 3% -> 3%
where the time goes in v5:
time: 163 us
  Pallas kernels  126 us (77%)
  local copies, waits for them, and re-layouts  20.6 us (13%)
  other arithmetic  11.2 us (7%)
  waiting for transfers between devices  2.65 us (2%)
  starting transfers between devices  2.4 us (1%)
    pallas_call x1, Pallas kernels, gathered(): pl.pallas_call(functools.partial(gather_kernel, group, n, starts), out_sh...  95.6 us
    pallas_call x1, Pallas kernels, finished(): pl.pallas_call(functools.partial(outside_kernel, dims, levels, used, grou...  19.5 us
    unnamed x36, local copies, waits for them, and re-layouts  11.8 us
    pallas_call x2, Pallas kernels, per_block(): pl.pallas_call(kernel, grid=(group,), out_shape=outs, in_specs=specs, out...  10.5 us
  transfers between devices with their start and end apart: 4, of which 1 were waited for; matrix products, arithmetic and copies ran while one was open for 7% of the time, Pallas kernels for 3%

profile of v5, /device:TPU:0, one launch (start us, length us, event | category | flops | bytes accessed | tf_op | source)
XLA Modules:
  0.0 162.7 jit_solution(4345969040994492977)
XLA Ops:
  0.0 0.8 slice.80
  1.6 1.7 %copy.13 = bf16[1,128,4640]{2,1,0:T(8,128)(2,1)S(1)} copy(bf16[1,128,4640]{1,2,0:T(8,128)(2,1)} %param.12) | data formatting | bytes 2375680 | tf_op args[1]
  4.6 1.3 fusion.2.u_ref
  5.9 0.8 fusion.14.tail_ref
  6.7 95.6 %shard_map.109 = (bf16[4,256,1408]{2,1,0:T(8,128)(2,1)}, bf16[16,1408]{1,0:T(8,128)(2,1)}) custom-call(bf16[256,2048]{1,0:T(8,128)(2,1)} %fusion.2.u_ref, bf16[128,4640]{1,0:T(8,128)(2,1)} %bitcast.87, bf16[4,128,128]{2,1,0:T(8,128)(2,1)} %fusion.14.tail_ref), custom_call_target="tpu_custom_call" | custom-call | tf_op jit(solution)/shard_map/pallas_call | solution.py:369
  102.3 1.8 %copy-done.1 = bf16[4,256,1408]{2,1,0:T(8,128)(2,1)S(1)} copy-done((bf16[4,256,1408]{2,1,0:T(8,128)(2,1)S(1)}, bf16[4,256,1408]{2,1,0:T(8,128)(2,1)}, u32[]{:S(2)}) %copy-start.1) | copy-done | bytes 2883608
  104.1 0.8 copy-done.7
  104.9 6.3 %shard_map.110 = (bf16[4,256,512]{2,1,0:T(8,128)(2,1)S(1)}, bf16[4,256,256]{2,1,0:T(8,128)(2,1)S(1)}, f32[4,256,128]{2,1,0:T(8,128)S(1)}, f32[4,256,128]{2,1,0:T(8,128)S(1)}, f32[4,128,512]{2,1,0:T(8,128)S(1)}) custom-call(bf16[4,256,1408]{2,1,0:T(8,128)(2,1)S(1)} %copy-done.1, bf16[4,256,1408]{2,1,0:T(8,128)(2,1)S(1)} %copy-done.1, ...), custom_call_target="tpu_custom_call" | custom-call | flops 134217728 | bytes 5828608 | tf_op jit(solution)/shard_map/pallas_call | solution.py:622
  111.2 0.8 copy-done.4
  112.0 1.0 copy-done.9
  113.6 2.3 %collective-permute-start.1 = (f32[8]{0:T(128)}, f32[8]{0:T(128)}, u32[]{:S(2)}, u32[]{:S(2)}) collective-permute-start(f32[8]{0:T(128)} %get-tuple-element.22), channel_id=1, source_target_pairs={{0,4},{4,0},{1,5},{5,1},{2,6},{6,2},{3,7},{7,3},{8,12},{12,8},{9,1... | collective-permute-start | bytes 104 | tf_op jit(solution)/shard_map/ppermute | solution.py:678
  117.0 0.8 fusion.25
  123.4 0.8 exp.122.fade_ref
  125.9 1.2 fusion.17
  127.9 1.6 %fusion.15 = (bf16[1,128,512]{2,1,0:T(8,128)(2,1)S(1)}, bf16[128,512]{1,0:T(8,128)(2,1)}) fusion(bf16[128,512]{1,0:T(8,128)(2,1)} %collective-permute-done, pred[]{:T(512)S(6)} %eq.6, f32[128,512]{1,0:T(8,128)S(1)} %get-tuple-element.24, f32[512]{0:T(512)} %exp.120, f32[512]{0:T(512)} %exp.118), kind=kLoop, calls=%fused_computation.34 | loop fusion | flops 589824 | bytes 659457 | tf_op jit(solution)/shard_map/stack | solution.py:812
  129.6 1.0 copy-done.5
  130.6 1.2 copy-done.10
  131.8 4.2 %shard_map.111.y_ref = f32[4,256,512]{2,1,0:T(8,128)S(1)} custom-call(bf16[4,256,512]{2,1,0:T(8,128)(2,1)S(1)} %copy-done.10, bf16[4,256,256]{2,1,0:T(8,128)(2,1)S(1)} %get-tuple-element.15.bc_ref, f32[4,256,128]{2,1,0:T(8,128)S(1)} %copy-done.5, f32[4,256,128]{2,1,0:T(8,128)S(1)} %get-tuple-element.17.cum_ref, f32[1,512]{1,0:T(1,128)S(1)} %broadcast_in_dim_reshape.3.skip_ref), custom_call_target="tpu_custom_call" | custom-call | flops 2147483648 | bytes 2623488 | tf_op jit(solution)/shard_map/pallas_call | solution.py:622
  136.0 1.4 copy-done.3
  137.5 0.9 fusion.12
  138.5 1.0 copy-done.6
  139.6 19.5 %shard_map.112 = bf16[256,2048]{1,0:T(8,128)(2,1)S(1)} custom-call(f32[4,256,512]{2,1,0:T(8,128)} %copy-done.3, bf16[4,256,256]{2,1,0:T(8,128)(2,1)S(1)} %get-tuple-element.15.bc_ref, bf16[4,2,128,512]{3,2,1,0:T(8,128)(2,1)S(1)} %pad_maximum_fusion.near_ref, bf16[2,128,512]{2,1,0:T(8,128)(2,1)S(1)} %pad_maximum_fusion.1.far_ref, ...), custom_call_target="tpu_custom_call" | custom-call | tf_op jit(solution)/shard_map/pallas_call | solution.py:580
  159.1 2.6 %collective-permute-done.3 = bf16[256,2048]{1,0:T(8,128)(2,1)S(1)} collective-permute-done((bf16[256,2048]{1,0:T(8,128)(2,1)S(1)}, bf16[256,2048]{1,0:T(8,128)(2,1)S(1)}, u32[]{:S(2)}, u32[]{:S(2)}) %collective-permute-start.3) | collective-permute-done | bytes 1048608 | tf_op jit(solution)/shard_map/ppermute | solution.py:684
  161.8 1.0 copy.19
  (85 shorter events, 12.0 us)
Async XLA Ops:
  0.0 4.5 %copy-start = (f32[1,256]{1,0:T(1,128)S(1)}, f32[1,256]{1,0:T(1,128)}, u32[]{:S(2)}) copy-start(f32[1,256]{1,0:T(1,128)} %param.19) | copy-start | bytes 3076
  0.0 3.9 %slice-start.1 = ((f32[1,2304]{1,0:T(1,128)}), f32[1,2048]{1,0:T(1,128)S(1)}, s32[]{:S(2)}) async-start(f32[1,2304]{1,0:T(1,128)} %param.15), calls=%async_computation.1 | async-start | bytes 16384 | tf_op jit(solution)/shard_map/slice | solution.py:743
  0.0 3.9 %slice-start = ((f32[1,2304]{1,0:T(1,128)}), f32[1,256]{1,0:T(1,128)S(1)}, s32[]{:S(2)}) async-start(f32[1,2304]{1,0:T(1,128)} %param.15), calls=%async_computation | async-start | bytes 2048 | tf_op jit(solution)/shard_map/slice | solution.py:743
  0.0 3.4 %copy-start.16 = (f32[1,32]{1,0:T(1,128)S(1)}, f32[1,32]{1,0:T(1,128)}, u32[]{:S(2)}) copy-start(f32[1,32]{1,0:T(1,128)} %param.17) | copy-start | bytes 388
  0.0 3.4 %copy-start.15 = (f32[1,32]{1,0:T(1,128)S(1)}, f32[1,32]{1,0:T(1,128)}, u32[]{:S(2)}) copy-start(f32[1,32]{1,0:T(1,128)} %param.16) | copy-start | bytes 388
  0.0 3.5 %copy-start.2 = (bf16[1,256,2048]{2,1,0:T(8,128)(2,1)S(1)}, bf16[1,256,2048]{2,1,0:T(8,128)(2,1)}, u32[]{:S(2)}) copy-start(bf16[1,256,2048]{2,1,0:T(8,128)(2,1)} %param.11) | copy-start | bytes 3145732
  1.6 3.1 %copy-start.13 = (f32[1,2048]{1,0:T(1,128)S(1)}, f32[1,2048]{1,0:T(1,128)}, u32[]{:S(2)}) copy-start(f32[1,2048]{1,0:T(1,128)} %param.20) | copy-start | bytes 24580
  3.3 3.4 %copy-start.11 = (bf16[1,128,4640]{2,1,0:T(8,128)(2,1)}, bf16[1,128,4640]{2,1,0:T(8,128)(2,1)S(1)}, u32[]{:S(2)}) copy-start(bf16[1,128,4640]{2,1,0:T(8,128)(2,1)S(1)} %copy.13) | copy-start | bytes 3563524
  102.3 1.8 %copy-start.1 = (bf16[4,256,1408]{2,1,0:T(8,128)(2,1)S(1)}, bf16[4,256,1408]{2,1,0:T(8,128)(2,1)}, u32[]{:S(2)}) copy-start(bf16[4,256,1408]{2,1,0:T(8,128)(2,1)} %get-tuple-element.12.p_ref.before_ref) | copy-start | bytes 8650756
  104.1 0.8 copy-start.7
  111.2 0.8 copy-start.4
  112.0 1.0 copy-start.9
  113.6 12.3 %collective-permute-start.1 = (f32[8]{0:T(128)}, f32[8]{0:T(128)}, u32[]{:S(2)}, u32[]{:S(2)}) collective-permute-start(f32[8]{0:T(128)} %get-tuple-element.22), channel_id=1, source_target_pairs={{0,4},{4,0},{1,5},{5,1},{2,6},{6,2},{3,7},{7,3},{8,12},{12,8},{9,1... | collective-permute-start | bytes 104 | tf_op jit(solution)/shard_map/ppermute | solution.py:678
  117.0 2.1 %copy-start.12 = (f32[512]{0:T(512)}, f32[512]{0:T(512)S(1)}, u32[]{:S(2)}) copy-start(f32[512]{0:T(512)S(1)} %exp.105) | copy-start | bytes 6148
  117.7 10.2 %collective-permute-start = (bf16[128,512]{1,0:T(8,128)(2,1)}, bf16[128,512]{1,0:T(8,128)(2,1)}, u32[]{:S(2)}, u32[]{:S(2)}) collective-permute-start(bf16[128,512]{1,0:T(8,128)(2,1)} %get-tuple-element.23), channel_id=1, source_target_pairs={{0,4},{4,0},{1,5},{5,1},{2,6},{6,2},{3,7},{7,3},{8,12},{12,8},{9,1... | collective-permute-start | bytes 393224 | tf_op jit(solution)/shard_map/ppermute | solution.py:678
  129.5 8.0 %collective-permute-start.2 = (bf16[128,512]{1,0:T(8,128)(2,1)}, bf16[128,512]{1,0:T(8,128)(2,1)}, u32[]{:S(2)}, u32[]{:S(2)}) collective-permute-start(bf16[128,512]{1,0:T(8,128)(2,1)} %get-tuple-element.33), channel_id=1, source_target_pairs={{0,8},{8,0},{1,9},{9,1},{2,10},{10,2},{3,11},{11,3},{4,12},{12,4},... | collective-permute-start | bytes 393224 | tf_op jit(solution)/shard_map/ppermute | solution.py:678
  129.5 1.0 copy-start.5
  130.6 1.2 copy-start.10
  131.8 5.6 %copy-start.14 = (f32[8]{0:T(128)S(1)}, f32[8]{0:T(128)}, u32[]{:S(2)}) copy-start(f32[8]{0:T(128)} %get-tuple-element.34) | copy-start | bytes 100
  131.8 6.7 %copy-start.8 = (f32[1,2048]{1,0:T(1,128)S(1)}, f32[1,2048]{1,0:T(1,128)}, u32[]{:S(2)}) copy-start(f32[1,2048]{1,0:T(1,128)} %param.21) | copy-start | bytes 24580
  136.0 1.4 copy-start.3
  138.5 1.0 copy-start.6
  159.0 2.7 %collective-permute-start.3 = (bf16[256,2048]{1,0:T(8,128)(2,1)S(1)}, bf16[256,2048]{1,0:T(8,128)(2,1)S(1)}, u32[]{:S(2)}, u32[]{:S(2)}) collective-permute-start(bf16[256,2048]{1,0:T(8,128)(2,1)S(1)} %shard_map.112), channel_id=1, source_target_pairs={{0,16},{16,0},{1,17},{17,1},{2,18},{18,2},{3,19},{19,3},{4,20},{20... | collective-permute-start | bytes 3145736 | tf_op jit(solution)/shard_map/ppermute | solution.py:684
